TPU v7x, 32 devices: a 4x4x1 block of a 4x4x8 slice. The times are simulated.
32 devices in a mesh: dp: 1 (over z), depth: 4 (over y), col: 4 (over x), row: 2 (over core).
Axes of the slice: x: 4, y: 4, z: 1, core: 2. Of those that a mesh axis runs over, the one named last changes fastest.
The devices are a block of a 4x4x8 slice.
Arguments:
- x_in: bfloat16 [16384, 2048], P(('dp', 'depth', 'row'), 'col')
- ln_gamma: float32 [2048], P('col')
- ln_beta: float32 [2048], P('col')
- w_up: bfloat16 [2048, 8192], P('row', 'col')
- b_up: bfloat16 [8192], P('col')
- w_down: bfloat16 [8192, 2048], P('row', 'col')
- b_down: bfloat16 [2048], P('col')
- grad_out: bfloat16 [16384, 2048], P(('dp', 'depth', 'row'), 'col')
Outputs:
- output 1: bfloat16 [16384, 2048], P(('dp', 'depth', 'row'), 'col')
- output 2: bfloat16 [16384, 2048], P(('dp', 'depth', 'row'), 'col')
- output 3: float32 [2048], P(('dp', 'col'))
- output 4: float32 [2048], P(('dp', 'col'))
- output 5: bfloat16 [2048, 8192], P(('dp', 'row'), 'col')
- output 6: float32 [8192], P(('dp', 'col'))
- output 7: bfloat16 [8192, 2048], P(('dp', 'row'), 'col')
- output 8: float32 [2048], P(('dp', 'col'))
All inputs are finite; a program needn't handle non-finite values.
Results may differ from a plain program's by a relative error of at most 0.0111579.
Values are sent between devices in bfloat16 or wider.
A program may use at most 768 MiB of HBM per device.

v0:
```python
import jax
import jax.numpy as jnp
from jax import lax
from jax.sharding import PartitionSpec as P

LN_EPS = 1e-5


def gelu_tanh(values):
    return jax.nn.gelu(values, approximate=True)


def solution(mesh):
    col_size = mesh.shape['col']
    token_axes = ('depth', 'row')
    tok_spec = P(('dp', 'depth', 'row'), 'col')
    vec_spec = P('col')
    mat_spec = P('row', 'col')
    grad_vec = P(('dp', 'col'))
    grad_mat = P(('dp', 'row'), 'col')

    def local_pass(x_blk, gamma_blk, beta_blk, w_up_blk, b_up_blk, w_down_blk, b_down_blk, dy_blk):
        inv_width = 1.0 / (x_blk.shape[1] * col_size)
        x_f32 = x_blk.astype(jnp.float32)
        row_mean = lax.psum(jnp.sum(x_f32, axis=1, keepdims=True), 'col') * inv_width
        centered = x_f32 - row_mean
        row_var = lax.psum(jnp.sum(centered * centered, axis=1, keepdims=True), 'col') * inv_width
        inv_std = lax.rsqrt(row_var + LN_EPS)
        x_hat = centered * inv_std
        x_norm = (x_hat * gamma_blk + beta_blk).astype(jnp.bfloat16)
        norm_rows = lax.all_gather(x_norm, 'col', axis=1, tiled=True)
        w_up_cols = lax.all_gather(w_up_blk, 'row', axis=0, tiled=True)
        pre_act = (jnp.dot(norm_rows, w_up_cols, preferred_element_type=jnp.float32) + b_up_blk.astype(jnp.float32)).astype(jnp.bfloat16)
        act_f32, gelu_vjp = jax.vjp(gelu_tanh, pre_act.astype(jnp.float32))
        hidden = act_f32.astype(jnp.bfloat16)
        hidden_rows = lax.all_gather(hidden, 'col', axis=1, tiled=True)
        w_down_cols = lax.all_gather(w_down_blk, 'row', axis=0, tiled=True)
        y_blk = (x_f32 + jnp.dot(hidden_rows, w_down_cols, preferred_element_type=jnp.float32) + b_down_blk.astype(jnp.float32)).astype(jnp.bfloat16)
        dy_f32 = dy_blk.astype(jnp.float32)
        grad_b_down = lax.psum(jnp.sum(dy_f32, axis=0), token_axes)
        down_part = jnp.einsum('tf,th->fh', hidden_rows, dy_blk, preferred_element_type=jnp.float32)
        grad_w_down = lax.psum(lax.psum_scatter(down_part, 'row', scatter_dimension=0, tiled=True), 'depth').astype(jnp.bfloat16)
        hidden_part = jnp.einsum('th,fh->tf', dy_blk, w_down_cols, preferred_element_type=jnp.float32)
        grad_hidden = lax.psum_scatter(hidden_part, 'col', scatter_dimension=1, tiled=True)
        grad_pre = gelu_vjp(grad_hidden)[0].astype(jnp.bfloat16)
        grad_b_up = lax.psum(jnp.sum(grad_pre.astype(jnp.float32), axis=0), token_axes)
        up_part = jnp.einsum('th,tf->hf', norm_rows, grad_pre, preferred_element_type=jnp.float32)
        grad_w_up = lax.psum(lax.psum_scatter(up_part, 'row', scatter_dimension=0, tiled=True), 'depth').astype(jnp.bfloat16)
        norm_part = jnp.einsum('tf,hf->th', grad_pre, w_up_cols, preferred_element_type=jnp.float32)
        grad_norm = lax.psum_scatter(norm_part, 'col', scatter_dimension=1, tiled=True)
        grad_gamma = lax.psum(jnp.sum(grad_norm * x_hat, axis=0), token_axes)
        grad_beta = lax.psum(jnp.sum(grad_norm, axis=0), token_axes)
        grad_hat = grad_norm * gamma_blk
        sum_plain, sum_proj = lax.psum((jnp.sum(grad_hat, axis=1, keepdims=True), jnp.sum(grad_hat * x_hat, axis=1, keepdims=True)), 'col')
        grad_x = (dy_f32 + inv_std * (grad_hat - sum_plain * inv_width - x_hat * (sum_proj * inv_width))).astype(jnp.bfloat16)
        return y_blk, grad_x, grad_gamma, grad_beta, grad_w_up, grad_b_up, grad_w_down, grad_b_down

    return jax.shard_map(
        local_pass,
        mesh=mesh,
        in_specs=(tok_spec, vec_spec, vec_spec, mat_spec, vec_spec, mat_spec, vec_spec, tok_spec),
        out_specs=(tok_spec, tok_spec, grad_vec, grad_vec, grad_mat, grad_vec, grad_mat, grad_vec),
        check_vma=False,
    )
```

profile of v0, /device:TPU:96, one launch (start us, length us, event | category | flops | bytes accessed | tf_op | source)
XLA Modules:
  0.0 1568.8 jit_solution(14981121502774673293)
XLA Ops:
  7.2 0.0 copy-start
  7.2 0.0 copy-start.7
  7.2 0.1 all-gather.11.cloned.1.call-start
  7.3 0.7 all-gather.11.cloned.1.call-update
  8.0 0.1 all-gather.7.cloned.1.call-start
  8.1 0.7 all-gather.7.cloned.1.call-update
  8.8 0.1 all-gather.5.cloned.1.call-start
  8.9 0.0 copy-done
  8.9 0.3 convert_reduce_fusion.1
  9.3 10.4 psum.70
  19.7 0.0 copy-start.3
  19.7 1.0 fusion.22
  20.8 7.9 psum.71
  28.7 0.0 copy-start.5
  28.7 0.6 copy-done.5
  29.3 1.9 fusion.17
  31.2 0.1 all-gather.5.cloned.1.call-update
  31.3 0.1 reduce-scatter.5.cloned.1.call-start
  31.3 1.7 all-gather.11.cloned.1.call-done
  33.0 31.1 %fusion.27 = f32[2048,8192]{1,0:T(8,128)} fusion(bf16[2048,512]{1,0:T(8,128)(2,1)} %param.15, bf16[8192,512]{1,0:T(8,128)(2,1)} %all-gather.11.cloned.1.call-done), kind=kOutput, calls=%fused_computation.43 | convolution fusion | flops 17179869184 | bytes 77594624 | tf_op jit(solution)/shard_map/th,fh->tf/dot_general | solution.py:43
  64.1 0.1 reduce-scatter.5.cloned.1.call-update
  64.1 0.2 all-gather.9.cloned.1.call-start
  64.4 0.4 copy-done.9
  64.8 76.6 %all-gather.5.cloned.1.call-done = bf16[2048,2048]{1,0:T(8,128)(2,1)} async-done(((bf16[2048,512]{1,0:T(8,128)(2,1)}), bf16[2048,2048]{1,0:T(8,128)(2,1)}) %all-gather.5.cloned.1.call-update) | async-done | bytes 8388624 | tf_op jit(solution)/shard_map/all_gather | solution.py:31
  141.3 553.1 %reduce-scatter.5.cloned.1.call-done = f32[2048,2048]{1,0:T(8,128)} async-done(((f32[2048,8192]{1,0:T(8,128)}), f32[2048,2048]{1,0:T(8,128)}) %reduce-scatter.5.cloned.1.call-update) | async-done | bytes 16777232 | tf_op jit(solution)/shard_map/reduce_scatter | solution.py:44
  694.4 37.6 %convert_reduce_fusion = (f32[2048]{0:T(1024)S(1)}, bf16[2048,2048]{1,0:T(8,128)(2,1)}, bf16[2048,2048]{1,0:T(8,128)(2,1)}) fusion(f32[2048,2048]{1,0:T(8,128)} %reduce-scatter.5.cloned.1.call-done, f32[2048]{0:T(1024)S(1)} %convert_element_type.44, bf16[2048,2048]{1,0:T(8,128)(2,1)} %all-gather.5.cloned.1.call-done, ...), kind=kOutput, calls=%fused_computation.15 | convolution fusion | flops 17293113344 | bytes 50348032 | tf_op jit(solution)/shard_map/dot_general | solution.py:33
  732.0 0.1 all-gather.9.cloned.1.call-update
  732.0 0.3 reduce-scatter.9.cloned.1.call-start
  732.3 24.3 %fusion.29 = f32[2048,2048]{1,0:T(8,128)} fusion(bf16[2048,2048]{1,0:T(8,128)(2,1)} %all-gather.5.cloned.1.call-done, bf16[2048,2048]{1,0:T(8,128)(2,1)} %get-tuple-element.21), kind=kOutput, calls=%fused_computation.45 | convolution fusion | flops 17179869184 | bytes 33554432 | tf_op jit(solution)/shard_map/th,tf->hf/dot_general | solution.py:47
  756.6 0.1 reduce-scatter.9.cloned.1.call-update
  756.7 0.1 reduce-scatter.7.cloned.1.call-start
  756.8 24.3 %fusion.28 = f32[2048,2048]{1,0:T(8,128)} fusion(bf16[2048,2048]{1,0:T(8,128)(2,1)} %get-tuple-element.21, bf16[2048,2048]{1,0:T(8,128)(2,1)} %all-gather.7.cloned.1.call-done), kind=kOutput, calls=%fused_computation.44 | convolution fusion | flops 17179869184 | bytes 33554432 | tf_op jit(solution)/shard_map/tf,hf->th/dot_general | solution.py:49
  781.1 0.1 reduce-scatter.7.cloned.1.call-update
  781.2 0.3 reduce-scatter.11.cloned.1.call-start
  781.5 242.1 %all-gather.9.cloned.1.call-done = bf16[2048,8192]{1,0:T(8,128)(2,1)} async-done(((bf16[2048,2048]{1,0:T(8,128)(2,1)}), bf16[2048,8192]{1,0:T(8,128)(2,1)}) %all-gather.9.cloned.1.call-update) | async-done | bytes 33554448 | tf_op jit(solution)/shard_map/all_gather | solution.py:36
  1023.6 27.0 %fusion.30 = f32[8192,512]{1,0:T(8,128)} fusion(bf16[2048,8192]{1,0:T(8,128)(2,1)} %all-gather.9.cloned.1.call-done, bf16[2048,512]{1,0:T(8,128)(2,1)S(1)} %copy-done.2), kind=kOutput, calls=%fused_computation.46 | convolution fusion | flops 17179869184 | bytes 52428800 | tf_op jit(solution)/shard_map/tf,th->fh/dot_general | solution.py:41
  1050.6 0.0 copy-start.8
  1050.6 0.1 reduce-scatter.11.cloned.1.call-update
  1050.7 0.6 copy-done.11
  1051.2 0.1 reduce-scatter.9.cloned.1.call-done
  1051.3 149.2 %reduce-scatter.7.cloned.1.call-done = f32[2048,512]{1,0:T(8,128)} async-done(((f32[2048,2048]{1,0:T(8,128)}), f32[2048,512]{1,0:T(8,128)}) %reduce-scatter.7.cloned.1.call-update) | async-done | bytes 4194320 | tf_op jit(solution)/shard_map/reduce_scatter | solution.py:50
  1200.6 0.0 copy-done.6
  1200.6 3.8 fusion.21
  1204.4 15.1 all-reduce.1
  1219.5 5.8 convert_reduce_fusion.2
  1225.3 24.5 %all-reduce = (f32[512]{0:T(512)}, f32[512]{0:T(512)}, f32[2048]{0:T(1024)}, f32[512]{0:T(512)}) all-reduce(f32[512]{0:T(512)S(1)} %get-tuple-element.8, f32[512]{0:T(512)S(1)} %get-tuple-element.11, f32[2048]{0:T(1024)S(1)} %get-tuple-element.20, ...), channel_id=1, replica_groups=mesh['dp'=1,'depth'=4,'col'=4,'row'=2] {'depth','row'}, use_global_device_ids=true, to_apply=%region_11.0 | all-reduce | flops 3584 | bytes 28672 | tf_op jit(solution)/shard_map/psum | solution.py:51
  1249.8 25.4 %fusion.25 = bf16[2048,512]{1,0:T(8,128)(2,1)} fusion(bf16[2048,512]{1,0:T(8,128)(2,1)S(1)} %copy-done.1, bf16[2048,8192]{1,0:T(8,128)(2,1)} %all-gather.9.cloned.1.call-done, bf16[8192,512]{1,0:T(8,128)(2,1)} %all-gather.11.cloned.1.call-done, f32[512]{0:T(512)S(1)} %convert_element_type.48), kind=kOutput, calls=%fused_computation.37 | convolution fusion | flops 17184063488 | bytes 46139392 | tf_op jit(solution)/shard_map/dot_general | solution.py:38
  1275.2 286.2 %all-reduce.4 = (bf16[1024,2048]{1,0:T(8,128)(2,1)}, bf16[4096,512]{1,0:T(8,128)(2,1)}) all-reduce(f32[1024,2048]{1,0:T(8,128)} %reduce-scatter.9.cloned.1.call-done, f32[4096,512]{1,0:T(8,128)} %reduce-scatter.11.cloned.1.call-done), channel_id=1, replica_groups=mesh['dp'=1,'depth'=4,'col'=4,'row'=2] {'depth'}, use_global_device_ids=true, to_apply=%region_15.0 | all-reduce | flops 4194304 | bytes 25165824 | tf_op jit(solution)/shard_map/psum | solution.py:48
  (21 shorter events, 0.1 us)
Async XLA Ops:
  7.2 1.7 copy-start
  7.2 22.1 %copy-start.10 = (f32[512]{0:T(512)S(1)}, f32[512]{0:T(512)}, u32[]{:S(2)}) copy-start(f32[512]{0:T(512)} %param.10) | copy-start | bytes 6148
  7.2 22.1 %copy-start.7 = (f32[512]{0:T(512)S(1)}, f32[512]{0:T(512)}, u32[]{:S(2)}) copy-start(f32[512]{0:T(512)} %param.9) | copy-start | bytes 6148
  7.2 25.8 %all-gather.11.cloned.1.call-start = ((), (), s32[]{:S(2)}) async-start(), calls=%async_computation.7 | async-start | bytes 12582912 | tf_op jit(solution)/shard_map/all_gather | solution.py:37
  8.0 56.7 %all-gather.7.cloned.1.call-start = ((), (), s32[]{:S(2)}) async-start(), calls=%async_computation.5 | async-start | bytes 12582912 | tf_op jit(solution)/shard_map/all_gather | solution.py:32
  8.8 132.5 %all-gather.5.cloned.1.call-start = ((), (), s32[]{:S(2)}) async-start(), calls=%async_computation.4 | async-start | bytes 10485760 | tf_op jit(solution)/shard_map/all_gather | solution.py:31
  19.7 44.3 %copy-start.3 = (f32[2048,1]{0,1:T(1,128)}, f32[2048,1]{0,1:T(1,128)S(1)}, u32[]{:S(2)}) copy-start(f32[2048,1]{0,1:T(1,128)S(1)} %broadcast_multiply_fusion.2) | copy-start | bytes 24580
  28.7 0.6 copy-start.5
  31.3 663.1 %reduce-scatter.5.cloned.1.call-start = ((), (), s32[]{:S(2)}) async-start(), calls=%async_computation.8 | async-start | bytes 83886080 | tf_op jit(solution)/shard_map/reduce_scatter | solution.py:44
  64.1 0.7 copy-start.9
  64.1 959.5 %all-gather.9.cloned.1.call-start = ((), (), s32[]{:S(2)}) async-start(), calls=%async_computation.6 | async-start | bytes 41943040 | tf_op jit(solution)/shard_map/all_gather | solution.py:36
  732.0 319.3 %reduce-scatter.9.cloned.1.call-start = ((), (), s32[]{:S(2)}) async-start(), calls=%async_computation.10 | async-start | bytes 25165824 | tf_op jit(solution)/shard_map/reduce_scatter | solution.py:48
  756.7 443.9 %reduce-scatter.7.cloned.1.call-start = ((), (), s32[]{:S(2)}) async-start(), calls=%async_computation.9 | async-start | bytes 20971520 | tf_op jit(solution)/shard_map/reduce_scatter | solution.py:50
  781.1 242.5 %copy-start.2 = (bf16[2048,512]{1,0:T(8,128)(2,1)S(1)}, bf16[2048,512]{1,0:T(8,128)(2,1)}, u32[]{:S(2)}) copy-start(bf16[2048,512]{1,0:T(8,128)(2,1)} %param.15) | copy-start | bytes 6291460
  781.2 494.0 %reduce-scatter.11.cloned.1.call-start = ((), (), s32[]{:S(2)}) async-start(), calls=%async_computation.11 | async-start | bytes 25165824 | tf_op jit(solution)/shard_map/reduce_scatter | solution.py:42
  1050.6 0.7 copy-start.11
  1050.6 150.0 %copy-start.1 = (bf16[2048,512]{1,0:T(8,128)(2,1)S(1)}, bf16[2048,512]{1,0:T(8,128)(2,1)}, u32[]{:S(2)}) copy-start(bf16[2048,512]{1,0:T(8,128)(2,1)} %param.8) | copy-start | bytes 6291460
  1050.6 150.0 %copy-start.4 = (f32[2048,1]{0,1:T(1,128)S(1)}, f32[2048,1]{0,1:T(1,128)}, u32[]{:S(2)}) copy-start(f32[2048,1]{0,1:T(1,128)} %copy-done.3) | copy-start | bytes 24580
  1050.6 150.0 %copy-start.6 = (f32[2048,1]{0,1:T(1,128)S(1)}, f32[2048,1]{0,1:T(1,128)}, u32[]{:S(2)}) copy-start(f32[2048,1]{0,1:T(1,128)} %copy-done.5) | copy-start | bytes 24580
  1050.6 150.0 %copy-start.8 = (f32[512]{0:T(512)S(1)}, f32[512]{0:T(512)}, u32[]{:S(2)}) copy-start(f32[512]{0:T(512)} %param.9) | copy-start | bytes 6148
Sparse Core Ops, SparseCore 0:
  9.6 23.3 all-gather.10
  34.5 22.2 all-gather.6
  59.0 82.2 all-gather.4
  143.5 550.7 reduce-scatter.4
  732.1 291.4 all-gather.8
  1025.8 25.5 reduce-scatter.8
  1053.7 146.8 reduce-scatter.6
  1202.9 24.2 reduce-scatter.10
where the time goes:
time: 1570 us
  waiting for transfers between devices  1020 us (65%)
  blocking collectives  344 us (22%)
  matrix products  170 us (11%)
    reduce_scatter x1, waiting for transfers between devices, local_pass(): lax.psum_scatter(hidden_part, 'col', scatter_dimension=1, tiled=True)  553 us
    psum x1, blocking collectives, local_pass(): lax.psum(lax.psum_scatter(up_part, 'row', scatter_dimension=0, tiled=True...  286 us
    all_gather x1, waiting for transfers between devices, local_pass(): hidden_rows = lax.all_gather(hidden, 'col', axis=1, tiled=True)  242 us
    reduce_scatter x1, waiting for transfers between devices, local_pass(): lax.psum_scatter(norm_part, 'col', scatter_dimension=1, tiled=True)  149 us
    all_gather x1, waiting for transfers between devices, local_pass(): norm_rows = lax.all_gather(x_norm, 'col', axis=1, tiled=True)  76.6 us
    dot_general x1, matrix products, local_pass(): jnp.dot(norm_rows, w_up_cols, preferred_element_type=jnp.float32)  37.6 us
  transfers between devices with their start and end apart: 8, of which 6 were waited for; matrix products, arithmetic and copies ran while one was open for 9% of the time, Pallas kernels for 0%

commit v1 on v0

v1 whole, which is shorter than its diff:
```python
import functools

import jax
import jax.numpy as jnp
from jax import lax
from jax.experimental import pallas as pl
from jax.experimental.pallas import tpu as pltpu
from jax.sharding import PartitionSpec as P

LN_EPS = 1e-5
F32 = jnp.float32
BF16 = jnp.bfloat16
MESH = pl.DeviceIdType.MESH
GELU_A = 0.7978845608028654
GELU_B = 0.044715
NCH = 4
ROWS = 16

NN = (((1,), (0,)), ((), ()))
NT = (((1,), (1,)), ((), ()))
TN = (((0,), (0,)), ((), ()))

SEMS = {}
for _z in ('x', 'g'):
    for _n in ('near', 'far', 'opp', 'd2d', 'd2o', 's_near', 's_far', 's_rel', 's_d2d'):
        SEMS[_z + _n] = NCH
    SEMS[_z + 'bounce'] = 2
for _p in ('y', 'd'):
    SEMS.update({_p + 's_give': 2, _p + 'got': 2, _p + 's_far': 1, _p + 'keep': 1, _p + 'far': 2, _p + 's_out': 4, _p + 'out': 1, _p + 'loc': 2})
SEMS.update(l_wu=1, s_wu=1, r_wu=1, s_wun=2, r_wun=1, s_wuy=4, r_wuy=4,
            s_wd0=2, s_wdx=4, r_wd=4, s_wdr=2, s_wdy=8, r_wdy=4,
            l_vec=2, s_vec=4, r_vec=2,
            ld=8, st=4, s_st=1, r_st=1,
            d_so=8, d_r=8, d_sa=8, d_p=8, d_sf=4, d_out=1, d_sy=8, d_y=2, d_sr=8, d_o=2,
            u_so=2, u_r=2, u_sa=2, u_p=2, u_sf=3, u_out=3, u_sr=1, u_o=2, l_small=2)
BASE = {}
_at = 0
for _n, _c in SEMS.items():
    BASE[_n] = _at
    _at += _c
N_SEM = _at


def gelu(v):
    return 0.5 * v * (1.0 + jnp.tanh(GELU_A * (v + GELU_B * (v * v * v))))


def gelu_slope(v):
    v2 = v * v
    t = jnp.tanh(GELU_A * (v + GELU_B * (v * v2)))
    return 0.5 * (1.0 + t) + 0.5 * v * (1.0 - t * t) * (GELU_A * (1.0 + 3.0 * GELU_B * v2))


def body(dims, x_ref, dy_ref, wu_ref, wd_ref, vec_ref, bu_ref,
         y_out, dx_out, gwu_out, gwd_out, cs_out, db_out,
         X, DY, XN, U, A, DU, YGOT, YFAR, YKEEP, GGOT, GFAR, GKEEP, PFD, PND, PFU, PNU,
         wu_v, wd_v, accD, accU, r1D, r2D, r1U, r2U, vec_v, bu_v, wb, fb, ob, finD, finU,
         db_v, cs_v, st_v, ms_v, st2_v, sx_v, sr_v, sem):
    TK, HB, FH = dims
    W, HW, TH, BLK, QF = 4 * HB, 2 * HB, TK // 2, TK // NCH, FH // 4
    RH, DQ, QH, DH, FB = W // 2, W // 4, FH // 8, W // 8, 2 * FH
    NTW = HB
    inv_w = 1.0 / W

    c, r, d = lax.axis_index('col'), lax.axis_index('row'), lax.axis_index('depth')
    c_odd, d_odd = lax.rem(c, 2), lax.rem(d, 2)
    cn, cf, co = c + 1 - 2 * c_odd, 3 - c, lax.rem(c + 2, 4)
    dn, df, do = d + 1 - 2 * d_odd, 3 - d, lax.rem(d + 2, 4)
    f, dh = lax.div(c, 2), lax.div(d, 2)
    tau = lax.rem(lax.div(c + 1, 2), 2)
    rp = 1 - r
    o, o2 = c_odd * FH, (1 - c_odd) * FH

    def S(name, i=0):
        return sem.at[BASE[name] + i]

    def ds(start, size):
        return pl.ds(pl.multiple_of(start, size), size)

    def dsm(start, size, mult):
        return pl.ds(pl.multiple_of(start, mult), size)

    def put(src, dst, ssem, rsem, **dev):
        pltpu.make_async_remote_copy(src_ref=src, dst_ref=dst, send_sem=ssem, recv_sem=rsem,
                                     device_id=dev, device_id_type=MESH).start()

    def copy(src, dst, s):
        pltpu.make_async_copy(src, dst, s).start()

    def wait(ref, s):
        pltpu.make_async_copy(ref, ref, s).wait()

    def loop(n, fn):
        def step(i, carry):
            fn(i)
            return carry
        lax.fori_loop(0, n, step, 0)

    bar = pltpu.get_barrier_semaphore()
    for dev in [dict(row=rp)] + [dict(row=h, **q) for h in range(2) for q in
                                 (dict(col=cn), dict(col=cf), dict(col=co), dict(depth=dn), dict(depth=df))]:
        pl.semaphore_signal(bar, inc=1, device_id=dev, device_id_type=MESH)
    pl.semaphore_wait(bar, 11)

    wun_src = lambda h: wu_ref.at[ds(d_odd * DQ, DQ), pl.ds(h * FH, FH)]
    wun_dst = wu_v.at[ds(d * DQ, DQ), ds(o, FH)]

    @pl.when(r == dh)
    def _():
        for h in range(2):
            put(wun_src(h), wun_dst, S('s_wun', h), S('r_wun'), col=cn, row=h)

    def wd_src(s, h):
        return wd_ref.at[dsm((2 * s + h) * FH + d * QF, QF, QF), :]

    def wd_dst(s, col):
        return wd_v.at[dsm(s * FH + d * QF, QF, QF), ds(col * HB, HB)]

    @pl.when(r == f)
    def _():
        for s in range(2):
            for h in range(2):
                put(wd_src(s, h), wd_dst(s, c), S('s_wdx', 2 * s + h), S('r_wd', 1), col=cn, row=h)
            copy(wd_src(s, r), wd_dst(s, c), S('r_wd', 0))
            put(wd_src(s, rp), wd_dst(s, c), S('s_wd0', s), S('r_wd', 0), row=rp)

    @pl.when(r != f)
    def _():
        for s in range(2):
            for h in range(2):
                put(wd_src(s, h), wd_dst(s, c), S('s_wdx', 2 * s + h), S('r_wd', 2), col=cf, row=h)

    copy(wu_ref.at[:, ds(r * FH, FH)], wu_v.at[ds(r * RH, RH), ds(o, FH)], S('l_wu'))
    put(wu_ref.at[:, ds(rp * FH, FH)], wu_v.at[ds(r * RH, RH), ds(o, FH)], S('s_wu'), S('r_wu'), row=rp)

    vec_at = vec_v.at[:, ds(c * HB, HB)]
    copy(vec_ref, vec_at, S('l_vec', 0))
    put(vec_ref, vec_at, S('s_vec', 0), S('r_vec', 0), col=cn)
    put(vec_ref, vec_at, S('s_vec', 1), S('r_vec', 0), col=cf)
    put(vec_ref, vec_at, S('s_vec', 2), S('r_vec', 0), col=co)
    bu_src, bu_at = bu_ref.at[:, ds(r * FH, FH)], bu_v.at[:, ds(o, FH)]
    copy(bu_src, bu_at, S('l_vec', 1))
    put(bu_src, bu_at, S('s_vec', 3), S('r_vec', 1), col=cn)

    def reg(Z, k, col):
        return Z.at[r, ds(k * BLK, BLK), ds(col * HB, HB)]

    def src_of(z_ref, k):
        return z_ref.at[ds(k * BLK, BLK), :]

    def send_own(z, z_ref, Z, which):
        def step(k):
            if 'near' in which:
                put(src_of(z_ref, k), reg(Z, k, c), S(z + 's_near', k), S(z + 'near', k), col=cn)
            if 'far' in which:
                put(src_of(z_ref, k), reg(Z, k, c), S(z + 's_far', k), S(z + 'far', k), col=cf)
            if 'd2d' in which:
                put(src_of(z_ref, k), reg(Z, k, c), S(z + 's_d2d', k), S(z + 'd2d', k), row=rp)
        loop(NCH, step)

    def d2d(z, Z, k, col, s):
        put(reg(Z, k, col), reg(Z, k, col), S(z + 's_d2d', k), S(z + s, k), row=rp)

    send_own('x', x_ref, X, ('near', 'far', 'd2d'))
    send_own('g', dy_ref, DY, ('near', 'd2d'))
    for i, z_ref in enumerate((x_ref, dy_ref)):
        for k in range(NCH):
            copy(z_ref.at[pl.ds(k * BLK, BLK), :], wb.at[i, :, pl.ds(k * HB, HB)], S('xg'[i] + 'bounce', 0))
    for i, Z in enumerate((X, DY)):
        wait(wb.at[i], S('xg'[i] + 'bounce', 0))
        for k in range(NCH):
            copy(wb.at[i, :, pl.ds(k * HB, HB)], reg(Z, k, c), S('xg'[i] + 'bounce', 1))

    db_v[...] = jnp.zeros_like(db_v)
    cs_v[...] = jnp.zeros_like(cs_v)

    for s in range(1):
        wait(wd_v.at[pl.ds(0, 2 * QF), pl.ds(0, HB)], S('r_wd', 2))
    for s in range(2):
        put(wd_dst(s, cf), wd_dst(s, cf), S('s_wdr', s), S('r_wd', 3), col=cn)

    def wuq(dd, half=None):
        if half is None:
            return wu_v.at[ds(dd * DQ, DQ), ds(o2, FH)]
        return wu_v.at[dsm(dd * DQ + half * DH, DH, DH), ds(o2, FH)]

    wait(wuq(d), S('r_wun'))
    put(wuq(d), wuq(d), S('s_wuy', 0), S('r_wuy', 0), depth=dn)
    put(wuq(d), wuq(d), S('s_wuy', 1), S('r_wuy', 1), depth=df)

    def wdq(s, dd, half=None):
        if half is None:
            return wd_v.at[dsm(s * FH + dd * QF, QF, QF), :]
        return wd_v.at[dsm(s * FH + dd * QF + half * QH, QH, QH), :]

    for i in (0, 1, 3):
        wait(wd_v.at[pl.ds(0, 2 * QF), pl.ds(0, HB)], S('r_wd', i))
    for s in range(2):
        put(wdq(s, d), wdq(s, d), S('s_wdy', s), S('r_wdy', 0), depth=dn)
        put(wdq(s, d), wdq(s, d), S('s_wdy', 2 + s), S('r_wdy', 1), depth=df)

    def x_near(k):
        wait(reg(X, k, cn), S('xnear', k))
        put(reg(X, k, cn), reg(X, k, cn), S('xs_rel', k), S('xopp', k), col=cf)
        d2d('x', X, k, cn, 'd2d')

    x_near(0)

    wait(wuq(dn), S('r_wuy', 0))
    put(wuq(dn, 1), wuq(dn, 1), S('s_wuy', 2), S('r_wuy', 3), depth=df)
    wait(wuq(df), S('r_wuy', 1))
    put(wuq(df, 0), wuq(df, 0), S('s_wuy', 3), S('r_wuy', 2), depth=dn)

    for i, Z in enumerate((X, DY)):
        wait(wb.at[i], S('xg'[i] + 'bounce', 1))
    wait(vec_at, S('l_vec', 0))
    wait(vec_v.at[:, pl.ds(0, 3 * HB)], S('r_vec', 0))
    wait(bu_at, S('l_vec', 1))
    wait(bu_at, S('r_vec', 1))
    wait(wu_v.at[ds(r * RH, RH), ds(o, FH)], S('l_wu'))
    wait(wu_v.at[ds(rp * RH, RH), ds(o, FH)], S('r_wu'))

    def norm_rows(buf, rows):
        xf = buf[rows, :].astype(F32)
        mean = jnp.sum(xf, axis=1, keepdims=True) * inv_w
        cen = xf - mean
        inv = lax.rsqrt(jnp.sum(cen * cen, axis=1, keepdims=True) * inv_w + LN_EPS)
        return cen, mean, inv

    def tok_of(s):
        return tau + s * (1 - 2 * tau)

    def w_relay():
        for s in range(1):
            wait(wd_v.at[pl.ds(0, 2 * QF), :], S('r_wdy', 0))
            wait(wd_v.at[pl.ds(0, 2 * QF), :], S('r_wdy', 1))
        for s in range(2):
            put(wdq(s, dn, 1), wdq(s, dn, 1), S('s_wdy', 4 + s), S('r_wdy', 3), depth=df)
            put(wdq(s, df, 0), wdq(s, df, 0), S('s_wdy', 6 + s), S('r_wdy', 2), depth=dn)

    def phase1(k):
        @pl.when(k < NCH - 1)
        def _():
            x_near(k + 1)

        @pl.when(k == 2)
        def _():
            send_own('g', dy_ref, DY, ('far',))
            w_relay()

        wait(reg(X, k, cf), S('xfar', k))
        d2d('x', X, k, cf, 'd2d')
        wait(reg(X, k, co), S('xopp', k))
        d2d('x', X, k, co, 'd2d')
        rows = ds(k * BLK, BLK)
        wait(X.at[rp, rows, :], S('xd2d', k))

        @pl.when(k == 0)
        def _():
            wait(wuq(do, 0), S('r_wuy', 2))
            wait(wuq(do, 1), S('r_wuy', 3))

        @pl.when(k > 0)
        def _():
            for s in range(2):
                wait(wb.at[s], S('st', s))
        for s in range(2):
            copy(X.at[tok_of(s), rows, :], wb.at[s], S('ld', s))

        def half(s):
            wait(wb.at[s], S('ld', s))

            def ln(i):
                rr = ds(i * ROWS, ROWS)
                cen, _, inv = norm_rows(wb.at[s], rr)
                wb[s, rr, :] = (cen * inv * vec_v[0:1, :] + vec_v[1:2, :]).astype(BF16)
            loop(BLK // ROWS, ln)
            copy(wb.at[s], XN.at[s, rows, :], S('st', s))

            @pl.when(k + s > 0)
            def _():
                wait(wb.at[2], S('st', 2))
                wait(wb.at[3], S('st', 3))

            def tile(n):
                cols = ds(s * o + n * NTW, NTW)
                acc = lax.dot_general(wb[s], wu_v[:, cols], NN, preferred_element_type=F32) + bu_v[0:1, cols]
                u = acc.astype(BF16)
                wb[2, :, cols] = u
                wb[3, :, cols] = gelu(u.astype(F32)).astype(BF16)
            loop((2 - s) * (FH // NTW), tile)
            copy(wb.at[2, :, pl.ds(0, FB)], U.at[s, rows, :], S('st', 2))
            copy(wb.at[3, :, pl.ds(0, FB)], A.at[s, rows, :], S('st', 3))
        loop(2, half)
    loop(NCH, phase1)
    for i in range(4):
        wait(wb.at[i], S('st', i))

    def g_near_far(k):
        wait(reg(DY, k, cf), S('gfar', k))
        put(reg(DY, k, cf), reg(DY, k, cf), S('gs_rel', k), S('gopp', k), col=cn)
        d2d('g', DY, k, cf, 'd2d')
        wait(reg(DY, k, cn), S('gnear', k))
        d2d('g', DY, k, cn, 'd2d')

    def g_opp(k):
        wait(reg(DY, k, co), S('gopp', k))
        d2d('g', DY, k, co, 'd2o')
        wait(reg(DY, k, co), S('gd2o', k))

    def tile_y(lhs, col):
        return lax.dot_general(lhs, wd_v[:, dsm(col, NTW, NTW)], NN, preferred_element_type=F32)

    def tile_g(lhs, col):
        return lax.dot_general(lhs, wu_v[dsm(col, NTW, NTW), :], NT, preferred_element_type=F32)

    def give(p, src, tile, GOT):
        def blk(b):
            return src.at[0, dsm(rp * TH + b * BLK, BLK, BLK), :]
        copy(blk(0), wb.at[0, :, pl.ds(0, FB)], S('ld', 0))

        def step(b):
            wait(wb.at[b, :, pl.ds(0, FB)], S('ld', b))

            @pl.when(b == 0)
            def _():
                copy(blk(1), wb.at[1, :, pl.ds(0, FB)], S('ld', 1))

            def half(h):
                @pl.when(b == 1)
                def _():
                    wait(fb.at[h], S(p + 's_give', h))

                def n_tile(n):
                    fb[h, :, ds(n * NTW, NTW)] = tile(wb[b, :, :FB], h * HW + n * NTW)
                loop(HW // NTW, n_tile)
                put(fb.at[h], GOT.at[ds(b * BLK, BLK), ds(h * HW, HW)], S(p + 's_give', h), S(p + 'got', b), row=rp)
            loop(2, half)
        loop(2, step)

    def keep(p, src, tile, GOT, FAR, KEEP):
        def blk(b):
            return src.at[0, dsm(r * TH + b * BLK, BLK, BLK), :]
        copy(blk(0), wb.at[0, :, pl.ds(0, FB)], S('ld', 0))
        for h in range(2):
            wait(fb.at[h], S(p + 's_give', h))

        def step(b):
            brow = ds(b * BLK, BLK)
            wait(GOT.at[brow, :], S(p + 'got', b))
            for h in range(2):
                col0 = (f if h else 1 - f) * HW
                copy(GOT.at[brow, ds(col0, HW)], fb.at[h], S('ld', 2 + h))
            wait(wb.at[b, :, pl.ds(0, FB)], S('ld', b))

            @pl.when(b == 0)
            def _():
                copy(blk(1), wb.at[1, :, pl.ds(0, FB)], S('ld', 1))

            def half(h):
                col0 = (1 - f + h * (2 * f - 1)) * HW

                @pl.when(jnp.logical_and(b == 1, h == 0))
                def _():
                    wait(fb.at[2], S(p + 's_far'))

                @pl.when(jnp.logical_and(b == 1, h == 1))
                def _():
                    wait(fb.at[3], S(p + 'keep'))

                def n_tile(n):
                    fb[2 + h, :, ds(n * NTW, NTW)] = tile(wb[b, :, :FB], col0 + n * NTW)
                loop(HW // NTW, n_tile)
                wait(fb.at[h], S('ld', 2 + h))

                def add(i):
                    rr = ds(i * ROWS, ROWS)
                    fb[2 + h, rr, :] = fb[2 + h, rr, :] + fb[h, rr, :]
                loop(BLK // ROWS, add)

                @pl.when(h == 0)
                def _():
                    put(fb.at[2], FAR.at[brow, :], S(p + 's_far'), S(p + 'far', b), col=cf)

                @pl.when(h == 1)
                def _():
                    copy(fb.at[3], KEEP.at[brow, :], S(p + 'keep'))
            loop(2, half)
        loop(2, step)

    def keep_end(p):
        wait(fb.at[2], S(p + 's_far'))
        wait(fb.at[3], S(p + 'keep'))

    def place(p, out, b):
        dst = out.at[dsm(r * TH + b * BLK, BLK, BLK), :]
        mine, other = ob.at[b, :, ds(c_odd * HB, HB)], ob.at[b, :, ds((1 - c_odd) * HB, HB)]
        put(other, dst, S(p + 's_out', 2 * b), S(p + 'out'), col=cn, row=tau)

        @pl.when(r == tau)
        def _():
            copy(mine, dst, S(p + 'loc', b))

        @pl.when(r != tau)
        def _():
            put(mine, dst, S(p + 's_out', 2 * b + 1), S(p + 'out'), row=rp)

    def place_end(p, b):
        wait(ob.at[b, :, pl.ds(0, HB)], S(p + 's_out', 2 * b))

        @pl.when(r == tau)
        def _():
            wait(ob.at[b, :, pl.ds(0, HB)], S(p + 'loc', b))

        @pl.when(r != tau)
        def _():
            wait(ob.at[b, :, pl.ds(0, HB)], S(p + 's_out', 2 * b + 1))

    fcols = ds(f * HW, HW)

    def y_final(b):
        brow = ds(b * BLK, BLK)
        wait(YFAR.at[brow, :], S('yfar', b))
        copy(YFAR.at[brow, :], fb.at[0], S('ld', 0))
        copy(YKEEP.at[brow, :], fb.at[1], S('ld', 1))
        copy(X.at[tau, dsm(r * TH + b * BLK, BLK, BLK), fcols], wb.at[0, :, pl.ds(0, HW)], S('ld', 2))
        wait(fb.at[0], S('ld', 0))
        wait(fb.at[1], S('ld', 1))
        wait(wb.at[0, :, pl.ds(0, HW)], S('ld', 2))

        def fin(i):
            rr = ds(i * ROWS, ROWS)
            ob[b, rr, :] = (wb[0, rr, :HW].astype(F32) + (fb[0, rr, :] + fb[1, rr, :]) + vec_v[2:3, fcols]).astype(BF16)
        loop(BLK // ROWS, fin)
        place('y', y_out, b)

    def da_block(k, s):
        rows = ds(k * BLK, BLK)
        copy(DY.at[tok_of(s), rows, :], wb.at[0], S('ld', 0))
        copy(U.at[s, rows, :], wb.at[1, :, pl.ds(0, FB)], S('ld', 1))
        wait(wb.at[0], S('ld', 0))
        wait(wb.at[1, :, pl.ds(0, FB)], S('ld', 1))

        @pl.when(k > 0)
        def _():
            wait(wb.at[2, :, pl.ds(0, FB)], S('st', 0))

        def tile(n):
            start = s * o + n * NTW
            cols = ds(start, NTW)
            da = lax.dot_general(wb[0], wd_v[ds(start, NTW), :], NT, preferred_element_type=F32)
            du = (da * gelu_slope(wb[1, :, cols].astype(F32))).astype(BF16)
            wb[2, :, cols] = du
            db_v[s, :, cols] += jnp.sum(du.astype(F32).reshape(BLK // 8, 8, NTW), axis=0)
        loop((2 - s) * (FH // NTW), tile)
        copy(wb.at[2, :, pl.ds(0, FB)], DU.at[s, rows, :], S('st', 0))

    def da_end():
        wait(wb.at[2, :, pl.ds(0, FB)], S('st', 0))

    def rows_of(kb):
        return ds(lax.rem(kb, NCH) * BLK, BLK), lax.div(kb, NCH)

    d_col = (c, cn, cf, co)

    def dwd_pass(js):
        def load(kb, slot):
            rows, s = rows_of(kb)
            copy(A.at[s, rows, ds(o, FH)], wb.at[slot, :, pl.ds(0, FH)], S('ld', slot))
            for i, j in enumerate(js):
                copy(DY.at[tok_of(s), rows, ds(d_col[j] * HB, HB)], wb.at[2 + slot, :, pl.ds(i * HB, HB)], S('ld', 2 + slot))
        for j in js:
            accD[j] = jnp.zeros((FH, HB), F32)
        load(0, 0)

        def step(kb):
            slot = lax.rem(kb, 2)

            @pl.when(kb < 2 * NCH - 1)
            def _():
                load(kb + 1, 1 - slot)
            wait(wb.at[slot, :, pl.ds(0, FH)], S('ld', slot))
            wait(wb.at[2 + slot, :, pl.ds(0, len(js) * HB)], S('ld', 2 + slot))
            for i, j in enumerate(js):
                accD[j] += lax.dot_general(wb[slot, :, :FH], wb[2 + slot, :, i * HB:(i + 1) * HB], TN, preferred_element_type=F32)
        loop(2 * NCH, step)

    def dwd_opp(j):
        put(accD.at[j, dsm(do * QF, QH, QH), :], r1D.at[j], S('d_so', 2 * j), S('d_r', 2 * j), depth=dn)
        put(accD.at[j, dsm(do * QF + QH, QH, QH), :], r2D.at[j], S('d_so', 2 * j + 1), S('d_r', 2 * j + 1), depth=df)

    def dwd_a(j):
        wait(r1D.at[j], S('d_r', 2 * j))
        rr = dsm(df * QF, QH, QH)
        accD[j, rr, :] += r1D[j]
        put(accD.at[j, ds(df * QF, QF), :], PFD.at[j], S('d_sa', 2 * j), S('d_p', 2 * j), depth=df)
        wait(r2D.at[j], S('d_r', 2 * j + 1))
        rr = dsm(dn * QF + QH, QH, QH)
        accD[j, rr, :] += r2D[j]
        put(accD.at[j, ds(dn * QF, QF), :], PND.at[j], S('d_sa', 2 * j + 1), S('d_p', 2 * j + 1), depth=dn)

    def dwd_rows(q, h, dd):
        return dsm((2 * q + h) * FH + dd * QF, QF, QF)

    def dwd_b(j):
        wait(PFD.at[j], S('d_p', 2 * j))
        wait(PND.at[j], S('d_p', 2 * j + 1))
        pf, pn = fb.at[0, pl.ds(0, QF), pl.ds(0, HB)], fb.at[1, pl.ds(0, QF), pl.ds(0, HB)]
        copy(PFD.at[j], pf, S('ld', 6))
        copy(PND.at[j], pn, S('ld', 7))
        wait(pf, S('ld', 6))
        wait(pn, S('ld', 7))
        finD[j] = (accD[j, ds(d * QF, QF), :] + (pf[...] + pn[...])).astype(BF16)
        dst = gwd_out.at[dwd_rows(c_odd, r, d), :]
        if j:
            put(finD.at[j], dst, S('d_sf', j), S('d_out'), col=d_col[j], row=f)
        else:
            @pl.when(r == f)
            def _():
                copy(finD.at[0], dst, S('d_out'))

            @pl.when(r != f)
            def _():
                put(finD.at[0], dst, S('d_sf', 0), S('d_out'), row=rp)

    def gwd(i, dd, half=None):
        if half is None:
            return gwd_out.at[dsm(i * FH + dd * QF, QF, QF), :]
        return gwd_out.at[dsm(i * FH + dd * QF + half * QH, QH, QH), :]

    def gwd_send():
        wait(gwd_out.at[pl.ds(0, 4 * QF), :], S('d_out'))
        for i in range(4):
            put(gwd(i, d), gwd(i, d), S('d_sy', i), S('d_y', 0), depth=dn)
            put(gwd(i, d), gwd(i, d), S('d_sy', 4 + i), S('d_y', 1), depth=df)

    def gwd_relay():
        wait(gwd_out.at[pl.ds(0, 4 * QF), :], S('d_y', 0))
        for i in range(4):
            put(gwd(i, dn, 1), gwd(i, dn, 1), S('d_sr', i), S('d_o', 1), depth=df)
        wait(gwd_out.at[pl.ds(0, 4 * QF), :], S('d_y', 1))
        for i in range(4):
            put(gwd(i, df, 0), gwd(i, df, 0), S('d_sr', 4 + i), S('d_o', 0), depth=dn)

    def dwu_part(dd):
        def load(kb, slot):
            rows, s = rows_of(kb)
            copy(XN.at[s, rows, ds(dd * DQ, DQ)], wb.at[slot, :, pl.ds(0, DQ)], S('ld', slot))
            copy(DU.at[s, rows, ds(o, FH)], wb.at[2 + slot, :, pl.ds(0, FH)], S('ld', 2 + slot))
        accU[dd] = jnp.zeros((DQ, FH), F32)
        load(0, 0)

        def step(kb):
            slot = lax.rem(kb, 2)

            @pl.when(kb < 2 * NCH - 1)
            def _():
                load(kb + 1, 1 - slot)
            wait(wb.at[slot, :, pl.ds(0, DQ)], S('ld', slot))
            wait(wb.at[2 + slot, :, pl.ds(0, FH)], S('ld', 2 + slot))
            accU[dd] += lax.dot_general(wb[slot, :, :DQ], wb[2 + slot, :, :FH], TN, preferred_element_type=F32)
        loop(2 * NCH, step)

    def dwu_opp():
        put(accU.at[do, pl.ds(0, DH), :], r1U, S('u_so', 0), S('u_r', 0), depth=dn)
        put(accU.at[do, pl.ds(DH, DH), :], r2U, S('u_so', 1), S('u_r', 1), depth=df)

    def dwu_a():
        wait(r1U, S('u_r', 0))
        accU[df, :DH, :] += r1U[...]
        put(accU.at[df], PFU, S('u_sa', 0), S('u_p', 0), depth=df)
        wait(r2U, S('u_r', 1))
        accU[dn, DH:, :] += r2U[...]
        put(accU.at[dn], PNU, S('u_sa', 1), S('u_p', 1), depth=dn)

    def dwu_parts(p):
        dd = jnp.where(p == 0, do, jnp.where(p == 1, df, jnp.where(p == 2, dn, d)))
        dwu_part(dd)

        @pl.when(p == 0)
        def _():
            dwu_opp()
            gwd_send()

        @pl.when(p == 2)
        def _():
            dwu_a()
            gwd_relay()

    def dwu_b():
        wait(PFU, S('u_p', 0))
        wait(PNU, S('u_p', 1))
        pf, pn = fb.at[0, :, pl.ds(0, FH)], fb.at[1, :, pl.ds(0, FH)]
        copy(PFU, pf, S('ld', 6))
        copy(PNU, pn, S('ld', 7))
        wait(pf, S('ld', 6))
        wait(pn, S('ld', 7))

        def fin(i):
            rr = ds(i * ROWS, ROWS)
            finU[rr, :] = (accU[d, rr, :] + (fb[0, rr, :FH] + fb[1, rr, :FH])).astype(BF16)
        loop(DQ // ROWS, fin)
        dst = gwu_out.at[ds(d_odd * DQ, DQ), ds(r * FH, FH)]
        put(finU, dst, S('u_sf', 0), S('u_out', 1), depth=dn, row=dh)
        put(finU, dst, S('u_sf', 1), S('u_out', 2), depth=df, row=dh)

        @pl.when(r == dh)
        def _():
            copy(finU, dst, S('u_out', 0))

        @pl.when(r != dh)
        def _():
            put(finU, dst, S('u_sf', 2), S('u_out', 0), row=rp)

    def gwu(start, size):
        return gwu_out.at[dsm(start, size, size), :]

    def gwu_relay():
        @pl.when(r == dh)
        def _():
            wait(gwu(lax.rem(dn, 2) * DQ, DQ), S('u_out', 1))
            part = gwu(lax.rem(dn, 2) * DQ + DH, DH)
            put(part, part, S('u_sr'), S('u_o', 1), depth=df)

        @pl.when(r != dh)
        def _():
            wait(gwu(lax.rem(df, 2) * DQ, DQ), S('u_out', 2))
            part = gwu(lax.rem(df, 2) * DQ, DH)
            put(part, part, S('u_sr'), S('u_o', 0), depth=dn)

    def gwu_end():
        @pl.when(r == dh)
        def _():
            wait(gwu(d_odd * DQ, DQ), S('u_out', 0))

        @pl.when(r != dh)
        def _():
            wait(gwu(0, DH), S('u_o', 0))
            wait(gwu(0, DH), S('u_o', 1))

    lane = lax.broadcasted_iota(jnp.int32, (ROWS, 128), 1)

    def dx_a(b):
        brow = ds(b * BLK, BLK)
        trow = dsm(r * TH + b * BLK, BLK, BLK)
        wait(GFAR.at[brow, :], S('dfar', b))
        copy(GFAR.at[brow, :], fb.at[0], S('ld', 0))
        copy(GKEEP.at[brow, :], fb.at[1], S('ld', 1))
        copy(X.at[tau, trow, :], wb.at[b], S('ld', 2))
        copy(DY.at[tau, trow, fcols], wb.at[2 + b, :, pl.ds(0, HW)], S('ld', 3))
        wait(fb.at[0], S('ld', 0))
        wait(fb.at[1], S('ld', 1))
        wait(wb.at[b], S('ld', 2))
        wait(wb.at[2 + b, :, pl.ds(0, HW)], S('ld', 3))

        def rows_step(i):
            rr = ds(i * ROWS, ROWS)
            _, mean, inv = norm_rows(wb.at[b], rr)
            xhat = (wb[b, rr, fcols].astype(F32) - mean) * inv
            dxn = fb[0, rr, :] + fb[1, rr, :]
            fb[2 + b, rr, :] = dxn
            gh = dxn * vec_v[0:1, fcols]
            s0 = jnp.sum(gh, axis=1, keepdims=True)
            s1 = jnp.sum(gh * xhat, axis=1, keepdims=True)
            srow = dsm(b * BLK + i * ROWS, ROWS, ROWS)
            st_v[srow, :] = jnp.where(lane < 64, s0, s1)
            ms_v[srow, :] = jnp.where(lane < 64, mean, inv)
            p1 = dxn * xhat
            cs_v[0] += jnp.sum(p1.reshape(ROWS // 8, 8, HW), axis=0)
            cs_v[1] += jnp.sum(dxn.reshape(ROWS // 8, 8, HW), axis=0)
        loop(BLK // ROWS, rows_step)

    NS = max(TH // 128, 1)
    SB = TH // NS

    def stats_send():
        for t in range(NS):
            tr = st_v[t * SB:(t + 1) * SB, :].T
            sx_v[t:t + 1, :SB] = tr[0:1, :]
            sx_v[NS + t:NS + t + 1, :SB] = tr[64:65, :]
        put(sx_v, sr_v, S('s_st'), S('r_st'), col=cf)

    def stats_recv():
        wait(sr_v, S('r_st'))
        for t in range(NS):
            for i in range(2):
                row = (sx_v[i * NS + t:i * NS + t + 1, :SB] + sr_v[i * NS + t:i * NS + t + 1, :SB]) * inv_w
                st2_v[i, t * SB:(t + 1) * SB, :] = jnp.broadcast_to(row, (128, SB)).T

    def dx_b(b):
        def rows_step(i):
            rr = ds(i * ROWS, ROWS)
            srow = dsm(b * BLK + i * ROWS, ROWS, ROWS)
            mean, inv = ms_v[srow, 0:1], ms_v[srow, 64:65]
            xhat = (wb[b, rr, fcols].astype(F32) - mean) * inv
            gh = fb[2 + b, rr, :] * vec_v[0:1, fcols]
            dx = wb[2 + b, rr, :HW].astype(F32) + inv * (gh - st2_v[0, srow, 0:1] - xhat * st2_v[1, srow, 0:1])
            ob[b, rr, :] = dx.astype(BF16)
        loop(BLK // ROWS, rows_step)
        place('d', dx_out, b)

    loop(2, g_near_far)
    wait(wd_v.at[pl.ds(0, 2 * QH), :], S('r_wdy', 2))
    wait(wd_v.at[pl.ds(0, 2 * QH), :], S('r_wdy', 3))
    give('y', A, tile_y, YGOT)
    g_near_far(2)
    keep('y', A, tile_y, YGOT, YFAR, YKEEP)
    g_near_far(3)

    def g_ready(k):
        wait(DY.at[rp, ds(k * BLK, BLK), pl.ds(0, 3 * HB)], S('gd2d', k))
    loop(NCH, g_ready)
    dwd_pass((0, 1, 2))
    for j in (0, 1, 2):
        dwd_opp(j)
    for j in (0, 1, 2):
        dwd_a(j)

    def da_t(k):
        g_opp(k)
        da_block(k, 0)
    loop(NCH, da_t)
    da_end()
    keep_end('y')
    for j in (0, 1, 2):
        dwd_b(j)
    dwd_pass((3,))
    dwd_opp(3)
    y_final(0)
    give('d', DU, tile_g, GGOT)
    dwd_a(3)
    keep('d', DU, tile_g, GGOT, GFAR, GKEEP)
    keep_end('d')
    dwd_b(3)
    loop(NCH, lambda k: da_block(k, 1))
    da_end()
    loop(4, dwu_parts)
    y_final(1)
    dwu_b()
    for b in range(2):
        place_end('y', b)
        dx_a(b)
    stats_send()
    stats_recv()
    for b in range(2):
        dx_b(b)
    gwu_relay()
    copy(cs_v, cs_out, S('l_small', 0))
    copy(db_v, db_out, S('l_small', 1))

    gwu_end()
    wait(gwd_out.at[pl.ds(0, 4 * QH), :], S('d_o', 0))
    wait(gwd_out.at[pl.ds(0, 4 * QH), :], S('d_o', 1))
    for p, out in (('y', y_out), ('d', dx_out)):
        @pl.when(r == tau)
        def _():
            wait(out.at[pl.ds(0, TH), :], S(p + 'out'))

        @pl.when(r != tau)
        def _():
            wait(out, S(p + 'out'))
    wait(cs_v, S('l_small', 0))
    wait(db_v, S('l_small', 1))
    for b in range(2):
        place_end('d', b)
    wait(sx_v, S('s_st'))

    @pl.when(r == dh)
    def _():
        for h in range(2):
            wait(wun_dst, S('s_wun', h))

    @pl.when(r == f)
    def _():
        for s in range(2):
            wait(wd_dst(0, c), S('s_wd0', s))
    for i in range(4):
        wait(wd_dst(0, c), S('s_wdx', i))
    wait(wu_v.at[ds(r * RH, RH), ds(o, FH)], S('s_wu'))
    for i in range(3):
        wait(vec_at, S('s_vec', i))
    wait(bu_at, S('s_vec', 3))
    for s in range(2):
        wait(wd_dst(s, cf), S('s_wdr', s))
    for i in range(2):
        wait(wuq(d), S('s_wuy', i))
        wait(wuq(d, 0), S('s_wuy', 2 + i))
    for i in range(4):
        wait(wdq(0, d), S('s_wdy', i))
        wait(wdq(0, d, 0), S('s_wdy', 4 + i))

    def sends(k):
        for z, Z in (('x', X), ('g', DY)):
            for n in ('s_near', 's_far', 's_rel'):
                wait(reg(Z, k, c), S(z + n, k))
            wait(Z.at[r, ds(k * BLK, BLK), :], S(z + 's_d2d', k))
    loop(NCH, sends)
    for i in range(8):
        wait(r1D.at[0], S('d_so', i))
        wait(PFD.at[0], S('d_sa', i))
        wait(gwd(0, d), S('d_sy', i))
        wait(gwd(0, d, 0), S('d_sr', i))
    for j in range(1, 4):
        wait(finD.at[j], S('d_sf', j))

    @pl.when(r != f)
    def _():
        wait(finD.at[0], S('d_sf', 0))
    for i in range(2):
        wait(r1U, S('u_so', i))
        wait(PFU, S('u_sa', i))
        wait(finU, S('u_sf', i))

    @pl.when(r != dh)
    def _():
        wait(finU, S('u_sf', 2))
    wait(gwu(0, DH), S('u_sr'))


def block_kernel(x, dy, wu, wd, vec, bu):
    (TK, HB), FH = x.shape, wu.shape[1] // 2
    W, HW, TH, BLK, QF, FB = 4 * HB, 2 * HB, TK // 2, TK // NCH, FH // 4, 2 * FH
    assert FB <= W and FH <= HW
    sd = jax.ShapeDtypeStruct
    NS = max(TH // 128, 1)
    outs = [sd((TK, HB), BF16), sd((TK, HB), BF16), sd((W // 2, FB), BF16), sd((4 * FH, HB), BF16), sd((2, 8, HW), F32), sd((2, 8, FB), F32)]
    n_out = len(outs)
    outs += [sd((2, TK, W), BF16)] * 3 + [sd((2, TK, FB), BF16)] * 3
    outs += [sd((TH, W), F32), sd((TH, HW), F32), sd((TH, HW), F32)] * 2
    outs += [sd((4, QF, HB), F32)] * 2 + [sd((W // 4, FH), F32)] * 2
    V = pltpu.VMEM
    scratch = [
        V((W, FB), BF16), V((FB, W), BF16), V((4, FH, HB), F32), V((4, W // 4, FH), F32),
        V((4, FH // 8, HB), F32), V((4, FH // 8, HB), F32), V((W // 8, FH), F32), V((W // 8, FH), F32),
        V((8, W), F32), V((8, FB), F32), V((4, BLK, W), BF16), V((4, BLK, HW), F32), V((2, BLK, HW), BF16),
        V((4, QF, HB), BF16), V((W // 4, FH), BF16), V((2, 8, FB), F32), V((2, 8, HW), F32),
        V((TH, 128), F32), V((TH, 128), F32), V((2, TH, 128), F32), V((2 * NS, 128), F32), V((2 * NS, 128), F32),
        pltpu.SemaphoreType.DMA((N_SEM,)),
    ]
    res = pl.pallas_call(
        functools.partial(body, (TK, HB, FH)),
        out_shape=outs,
        in_specs=[pl.BlockSpec(memory_space=pl.ANY)] * 6,
        out_specs=[pl.BlockSpec(memory_space=pl.ANY)] * len(outs),
        scratch_shapes=scratch,
        compiler_params=pltpu.CompilerParams(collective_id=0, has_side_effects=True, vmem_limit_bytes=67043328),
        name='mlp_block',
    )(x, dy, wu, wd, vec, bu)
    return res[:n_out]


def solution(mesh):
    assert (mesh.shape['col'], mesh.shape['row'], mesh.shape['depth']) == (4, 2, 4)
    tok_spec = P(('dp', 'depth', 'row'), 'col')
    vec_spec = P('col')
    mat_spec = P('row', 'col')
    grad_vec = P(('dp', 'col'))
    grad_mat = P(('dp', 'row'), 'col')
    near = [(i, i ^ 1) for i in range(4)]

    def local_pass(x_blk, gamma_blk, beta_blk, w_up_blk, b_up_blk, w_down_blk, b_down_blk, dy_blk):
        hb, fb = x_blk.shape[1], w_up_blk.shape[1]
        fh = fb // 2
        c, r = lax.axis_index('col'), lax.axis_index('row')
        vec = jnp.stack([gamma_blk, beta_blk, b_down_blk.astype(F32)] + [jnp.zeros_like(gamma_blk)] * 5)
        bu = jnp.broadcast_to(b_up_blk.astype(F32)[None], (8, fb))
        db_down = jnp.sum(dy_blk.astype(F32), axis=0)
        y_blk, dx_blk, grad_w_up, grad_w_down, cs, db = block_kernel(x_blk, dy_blk, w_up_blk, w_down_blk, vec, bu)
        cols = jnp.sum(cs, axis=1)
        mine = lax.dynamic_slice_in_dim(cols, (c % 2) * hb, hb, axis=1)
        other = lax.dynamic_slice_in_dim(cols, (1 - c % 2) * hb, hb, axis=1)
        cols = mine + lax.ppermute(other, 'col', near)
        db_up = jnp.sum(lax.dynamic_slice_in_dim(db, (c % 2) * fh, fh, axis=2), axis=(0, 1))
        db_up = lax.dynamic_update_slice_in_dim(jnp.zeros((fb,), F32), db_up, r * fh, axis=0)
        sums = lax.psum(jnp.concatenate([cols[0], cols[1], db_up, db_down]), ('depth', 'row'))
        return (y_blk, dx_blk, sums[:hb], sums[hb:2 * hb], grad_w_up, sums[2 * hb:2 * hb + fb], grad_w_down, sums[2 * hb + fb:])

    return jax.shard_map(
        local_pass,
        mesh=mesh,
        in_specs=(tok_spec, vec_spec, vec_spec, mat_spec, vec_spec, mat_spec, vec_spec, tok_spec),
        out_specs=(tok_spec, tok_spec, grad_vec, grad_vec, grad_mat, grad_vec, grad_mat, grad_vec),
        check_vma=False,
    )
```

time: 1570 us -> 821 us (0.52)
  waiting for transfers between devices: 1020 us -> 0.01 us
  Pallas kernels: 0 us -> 773 us
  blocking collectives: 344 us -> 23.6 us
  matrix products: 170 us -> 0 us
    pallas_call x0 -> x1, Pallas kernels: none -> 773 us  [block_kernel(): pl.pallas_call(functools.partial(body, (TK, HB, FH)), out_shape=outs, in_...]
    reduce_scatter x4 -> x0, waiting for transfers between devices: 702 us -> none  [the longest x1 553 us: local_pass(): lax.psum_scatter(hidden_part, 'col', scatter_dimension=1, tiled=True)]
    psum x5 -> x1, blocking collectives: 344 us -> 23.6 us  [local_pass(): lax.psum(jnp.concatenate([cols[0], cols[1], db_up, db_down]), ('depth', '...]
    all_gather x4 -> x0, waiting for transfers between devices: 320 us -> none  [the longest x1 242 us: local_pass(): hidden_rows = lax.all_gather(hidden, 'col', axis=1, tiled=True)]
    dot_general x6 -> x0, matrix products: 170 us -> none  [the longest x1 37.6 us: local_pass(): jnp.dot(norm_rows, w_up_cols, preferred_element_type=jnp.float32)]
  transfers between devices with their start and end apart: 8 -> 1, of which waited for: 6 -> 0; matrix products, arithmetic and copies ran while one was open for 9% -> 0% of each run, Pallas kernels for 0% -> 0%
where the time goes in v1:
time: 821 us; the launch traced here: 819 us
  Pallas kernels  773 us (94%)
  blocking collectives  23.6 us (3%)
  local copies, waits for them, and re-layouts  14.4 us (2%)
    pallas_call x1, Pallas kernels, block_kernel(): pl.pallas_call(functools.partial(body, (TK, HB, FH)), out_shape=outs, in_...  773 us
    psum x1, blocking collectives, local_pass(): lax.psum(jnp.concatenate([cols[0], cols[1], db_up, db_down]), ('depth', '...  23.6 us
  transfers between devices with their start and end apart: 1, of which 0 were waited for; matrix products, arithmetic and copies ran while one was open for 0% of the time, Pallas kernels for 0%

profile of v1, /device:TPU:96, one launch (start us, length us, event | category | flops | bytes accessed | tf_op | source)
XLA Modules:
  0.0 818.6 jit_solution(17817206374317380822)
XLA Ops:
  0.6 0.7 stack.24
  1.3 1.3 stack.23.vec_ref
  2.6 1.3 broadcast_in_dim.4.bu_ref
  4.0 772.7 %mlp_block.1 = (bf16[2048,512]{1,0:T(8,128)(2,1)}, bf16[2048,512]{1,0:T(8,128)(2,1)}, bf16[1024,2048]{1,0:T(8,128)(2,1)}, bf16[4096,512]{1,0:T(8,128)(2,1)}, f32...) custom-call(bf16[2048,512]{1,0:T(8,128)(2,1)} %x_ref.1, ...), custom_call_target="tpu_custom_call" | custom-call | tf_op jit(solution)/shard_map/mlp_block/pallas_call | solution.py:840
  776.7 0.0 copy-start.2
  776.7 1.0 reduce_sum.27
  777.7 2.6 collective-permute-start
  780.3 1.9 convert_reduce_fusion
  782.3 0.9 dynamic-slice_reduce_fusion
  783.2 0.3 dynamic_update_slice.3
  783.5 0.0 collective-permute-done
  783.5 23.6 %psum.7 = f32[3584]{0:T(1024)S(1)} all-reduce(f32[3584]{0:T(1024)S(1)} %pad_maximum_fusion), channel_id=1, replica_groups=mesh['dp'=1,'depth'=4,'col'=4,'row'=2] {'depth','row'}, use_global_device_ids=true, to_apply=%region_3.4 | all-reduce | flops 3584 | bytes 28672 | tf_op jit(solution)/shard_map/psum | solution.py:875
  807.1 0.6 fusion
  807.7 0.6 slice.28
  808.3 0.0 copy-start.1
  808.3 3.2 copy.21
  811.5 0.0 copy-done.2
  811.5 1.3 copy.22
  812.8 0.0 copy-done.1
  812.8 0.0 copy-start
  812.8 2.1 copy.23
  815.0 1.6 copy-done
  816.5 2.0 copy.24
  (7 shorter events, 0.0 us)
Async XLA Ops:
  776.7 34.9 %copy-start.2 = (bf16[2048,512]{1,0:T(8,128)(2,1)S(1)}, bf16[2048,512]{1,0:T(8,128)(2,1)}, u32[]{:S(2)}) copy-start(bf16[2048,512]{1,0:T(8,128)(2,1)} %get-tuple-element.34) | copy-start | bytes 6291460
  777.7 5.7 collective-permute-start
  808.3 4.5 copy-start.1
  812.8 3.7 copy-start

commit v2 on v1

v2 whole, which is shorter than its diff:
```python
import functools

import jax
import jax.numpy as jnp
from jax import lax
from jax.experimental import pallas as pl
from jax.experimental.pallas import tpu as pltpu
from jax.sharding import PartitionSpec as P

LN_EPS = 1e-5
F32 = jnp.float32
BF16 = jnp.bfloat16
MESH = pl.DeviceIdType.MESH
GELU_A = 0.7978845608028654
GELU_B = 0.044715
NCH = 4
ROWS = 16
LROWS = 64

NN = (((1,), (0,)), ((), ()))
NT = (((1,), (1,)), ((), ()))
TN = (((0,), (0,)), ((), ()))

SEMS = {}
for _z in ('x', 'g'):
    for _n in ('near', 'far', 'opp', 'd2d', 'd2o', 's_near', 's_far', 's_rel', 's_d2d'):
        SEMS[_z + _n] = NCH
    SEMS[_z + 'bounce'] = 2
for _p in ('y', 'd'):
    SEMS.update({_p + 's_give': 2, _p + 'got': 2, _p + 's_far': 2, _p + 'keep': 1, _p + 'far': 2, _p + 's_out': 4, _p + 'out': 1, _p + 'loc': 2})
SEMS.update(l_wu=1, s_wu=1, r_wu=1, s_wun=1, r_wun=1, s_wuy=4, r_wuy=4,
            s_wd0=2, s_wdx=4, r_wd=4, s_wdr=2, s_wdy=32, r_wdy=8,
            l_vec=2, s_vec=4, r_vec=2,
            ld=8, st=4, s_st=2, r_st=2, s_sum=4, r_sum=4,
            d_so=8, d_r=8, d_sa=8, d_p=8, d_sf=4, d_out=1, d_sy=8, d_y=2, d_sr=8, d_o=2,
            u_so=2, u_r=2, u_sa=2, u_p=2, u_sf=3, u_out=3, u_sr=1, u_o=2, l_small=2)
BASE = {}
_at = 0
for _n, _c in SEMS.items():
    BASE[_n] = _at
    _at += _c
N_SEM = _at


def gelu(v):
    return 0.5 * v * (1.0 + jnp.tanh(GELU_A * (v + GELU_B * (v * v * v))))


def gelu_slope(v):
    v2 = v * v
    t = jnp.tanh(GELU_A * (v + GELU_B * (v * v2)))
    return 0.5 * (1.0 + t) + 0.5 * v * (1.0 - t * t) * (GELU_A * (1.0 + 3.0 * GELU_B * v2))


def body(dims, x_ref, dy_ref, wu_ref, wd_ref, vec_ref, bu_ref,
         y_out, dx_out, gwu_out, gwd_out, sum_out,
         X, DY, XN, U, A, DU, YGOT, YFAR, YKEEP, GGOT, GFAR, GKEEP, PFD, PND, PFU, PNU,
         wu_v, wd_v, accD, accU, r1D, r2D, r1U, r2U, vec_v, bu_v, wb, fb, ob, finD,
         db_v, cs_v, st_v, ms_v, st2_v, sx_v, sr_v, bd_v, sum_v, sumr_v, sem):
    TK, HB, FH = dims
    W, HW, TH, BLK, QF = 4 * HB, 2 * HB, TK // 2, TK // NCH, FH // 4
    RH, DQ, QH, DH, FB = W // 2, W // 4, FH // 8, W // 8, 2 * FH
    NTW = HB
    inv_w = 1.0 / W
    finU = wb.at[3, pl.ds(0, DQ), pl.ds(HW, FH)]

    c, r, d = lax.axis_index('col'), lax.axis_index('row'), lax.axis_index('depth')
    c_odd, d_odd = lax.rem(c, 2), lax.rem(d, 2)
    cn, cf, co = c + 1 - 2 * c_odd, 3 - c, lax.rem(c + 2, 4)
    dn, df, do = d + 1 - 2 * d_odd, 3 - d, lax.rem(d + 2, 4)
    f, dh = lax.div(c, 2), lax.div(d, 2)
    tau = lax.rem(lax.div(c + 1, 2), 2)
    rp = 1 - r
    o, o2 = c_odd * FH, (1 - c_odd) * FH

    def S(name, i=0):
        return sem.at[BASE[name] + i]

    def ds(start, size):
        return pl.ds(pl.multiple_of(start, size), size)

    def dsm(start, size, mult):
        return pl.ds(pl.multiple_of(start, mult), size)

    def put(src, dst, ssem, rsem, **dev):
        pltpu.make_async_remote_copy(src_ref=src, dst_ref=dst, send_sem=ssem, recv_sem=rsem,
                                     device_id=dev, device_id_type=MESH).start()

    def copy(src, dst, s):
        pltpu.make_async_copy(src, dst, s).start()

    def wait(ref, s):
        pltpu.make_async_copy(ref, ref, s).wait()

    def loop(n, fn):
        def step(i, carry):
            fn(i)
            return carry
        lax.fori_loop(0, n, step, 0)

    bar = pltpu.get_barrier_semaphore()
    for dev in [dict(row=rp)] + [dict(row=h, **q) for h in range(2) for q in
                                 (dict(col=cn), dict(col=cf), dict(col=co), dict(depth=dn), dict(depth=df))]:
        pl.semaphore_signal(bar, inc=1, device_id=dev, device_id_type=MESH)
    pl.semaphore_wait(bar, 11)

    def wd_src(s, h):
        return wd_ref.at[dsm((2 * s + h) * FH + d * QF, QF, QF), :]

    def wd_dst(s, col):
        return wd_v.at[dsm(s * FH + d * QF, QF, QF), ds(col * HB, HB)]

    def reg(Z, k, col):
        return Z.at[r, ds(k * BLK, BLK), ds(col * HB, HB)]

    def send_own(z, z_ref, Z, which, chunks=(0, NCH)):
        def step(k):
            src = z_ref.at[ds(k * BLK, BLK), :]
            if 'near' in which:
                put(src, reg(Z, k, c), S(z + 's_near', k), S(z + 'near', k), col=cn)
            if 'far' in which:
                put(src, reg(Z, k, c), S(z + 's_far', k), S(z + 'far', k), col=cf)
            if 'd2d' in which:
                put(src, reg(Z, k, c), S(z + 's_d2d', k), S(z + 'd2d', k), row=rp)
        for k in range(*chunks):
            step(k)

    def d2d(z, Z, k, col, s):
        put(reg(Z, k, col), reg(Z, k, col), S(z + 's_d2d', k), S(z + s, k), row=rp)

    wu_own = wu_v.at[ds(r * RH, RH), ds(o, FH)]
    put(wu_ref.at[:, ds(rp * FH, FH)], wu_own, S('s_wu'), S('r_wu'), row=rp)
    copy(wu_ref.at[:, ds(r * FH, FH)], wu_own, S('l_wu'))

    @pl.when(r != f)
    def _():
        for s in range(2):
            for h in range(2):
                put(wd_src(s, h), wd_dst(s, c), S('s_wdx', 2 * s + h), S('r_wd', 2), col=cf, row=h)

    @pl.when(r == f)
    def _():
        for s in range(2):
            copy(wd_src(s, r), wd_dst(s, c), S('r_wd', 0))
            put(wd_src(s, rp), wd_dst(s, c), S('s_wd0', s), S('r_wd', 0), row=rp)

    send_own('x', x_ref, X, ('far', 'd2d'))
    send_own('g', dy_ref, DY, ('d2d',))
    for i, z_ref in enumerate((x_ref, dy_ref)):
        for k in range(NCH):
            copy(z_ref.at[pl.ds(k * BLK, BLK), :], wb.at[i, :, pl.ds(k * HB, HB)], S('xg'[i] + 'bounce', 0))

    vec_at = vec_v.at[:, ds(c * HB, HB)]
    copy(vec_ref, vec_at, S('l_vec', 0))
    put(vec_ref, vec_at, S('s_vec', 0), S('r_vec', 0), col=cn)
    put(vec_ref, vec_at, S('s_vec', 1), S('r_vec', 0), col=cf)
    put(vec_ref, vec_at, S('s_vec', 2), S('r_vec', 0), col=co)
    bu_src, bu_at = bu_ref.at[:, ds(r * FH, FH)], bu_v.at[:, ds(o, FH)]
    copy(bu_src, bu_at, S('l_vec', 1))
    put(bu_src, bu_at, S('s_vec', 3), S('r_vec', 1), col=cn)

    with jax.named_scope('wu_own'):
        wait(wu_own, S('l_wu'))
        wait(wu_v.at[ds(rp * RH, RH), ds(o, FH)], S('r_wu'))
    wun = wu_v.at[ds(d * DQ, DQ), ds(o, FH)]
    put(wun, wun, S('s_wun'), S('r_wun'), col=cn)

    @pl.when(r == f)
    def _():
        for s in range(2):
            for h in range(2):
                put(wd_src(s, h), wd_dst(s, c), S('s_wdx', 2 * s + h), S('r_wd', 1), col=cn, row=h)
    send_own('x', x_ref, X, ('near',), (0, 2))

    for i, Z in enumerate((X, DY)):
        wait(wb.at[i], S('xg'[i] + 'bounce', 0))
        for k in range(NCH):
            copy(wb.at[i, :, pl.ds(k * HB, HB)], reg(Z, k, c), S('xg'[i] + 'bounce', 1))

    db_v[...] = jnp.zeros_like(db_v)
    cs_v[...] = jnp.zeros_like(cs_v)
    bd_v[...] = jnp.zeros_like(bd_v)

    def dy_sum(i):
        rr = ds(i * ROWS, ROWS)
        part = jnp.sum(wb[1, rr, :].astype(F32).reshape(ROWS // 8, 8, W), axis=0)
        bd_v[...] += part[:, :HB] + part[:, HB:2 * HB] + part[:, 2 * HB:3 * HB] + part[:, 3 * HB:]
    loop(BLK // ROWS, dy_sum)

    with jax.named_scope('wd_far'):
        wait(wd_v.at[pl.ds(0, 2 * QF), pl.ds(0, HB)], S('r_wd', 2))
    for s in range(2):
        put(wd_dst(s, cf), wd_dst(s, cf), S('s_wdr', s), S('r_wd', 3), col=cn)
    send_own('x', x_ref, X, ('near',), (2, NCH))

    def wuq(dd, half=None):
        if half is None:
            return wu_v.at[ds(dd * DQ, DQ), ds(o2, FH)]
        return wu_v.at[dsm(dd * DQ + half * DH, DH, DH), ds(o2, FH)]

    with jax.named_scope('wu_near'):
        wait(wuq(d), S('r_wun'))
    put(wuq(d), wuq(d), S('s_wuy', 0), S('r_wuy', 0), depth=dn)
    put(wuq(d), wuq(d), S('s_wuy', 1), S('r_wuy', 1), depth=df)

    def wdq(s, dd, col, half=None):
        if half is None:
            return wd_v.at[dsm(s * FH + dd * QF, QF, QF), ds(col * HB, HB)]
        return wd_v.at[dsm(s * FH + dd * QF + half * QH, QH, QH), ds(col * HB, HB)]

    W_GROUPS = (((0, c), (1, cn), (2, cf)), ((3, co),))

    def wd_send(g):
        if g == 0:
            for i in (0, 1):
                wait(wd_v.at[pl.ds(0, 2 * QF), pl.ds(0, HB)], S('r_wd', i))
        else:
            wait(wd_v.at[pl.ds(0, 2 * QF), pl.ds(0, HB)], S('r_wd', 3))
        for i, col in W_GROUPS[g]:
            for s in range(2):
                put(wdq(s, d, col), wdq(s, d, col), S('s_wdy', 4 * i + s), S('r_wdy', 4 * g), depth=dn)
                put(wdq(s, d, col), wdq(s, d, col), S('s_wdy', 4 * i + 2 + s), S('r_wdy', 4 * g + 1), depth=df)

    def wd_bytes(g, rows):
        return wd_v.at[pl.ds(0, 2 * rows), pl.ds(0, len(W_GROUPS[g]) * HB)]

    def wd_relay(g):
        for i in range(2):
            wait(wd_bytes(g, QF), S('r_wdy', 4 * g + i))
        for i, col in W_GROUPS[g]:
            for s in range(2):
                put(wdq(s, dn, col, 1), wdq(s, dn, col, 1), S('s_wdy', 16 + 4 * i + s), S('r_wdy', 4 * g + 3), depth=df)
                put(wdq(s, df, col, 0), wdq(s, df, col, 0), S('s_wdy', 16 + 4 * i + 2 + s), S('r_wdy', 4 * g + 2), depth=dn)

    def x_near(k):
        wait(reg(X, k, cn), S('xnear', k))
        put(reg(X, k, cn), reg(X, k, cn), S('xs_rel', k), S('xopp', k), col=cf)
        d2d('x', X, k, cn, 'd2d')

    with jax.named_scope('x_near'):
        x_near(0)

    with jax.named_scope('wuy0'):
        wait(wuq(dn), S('r_wuy', 0))
    put(wuq(dn, 1), wuq(dn, 1), S('s_wuy', 2), S('r_wuy', 3), depth=df)
    with jax.named_scope('wuy1'):
        wait(wuq(df), S('r_wuy', 1))
    put(wuq(df, 0), wuq(df, 0), S('s_wuy', 3), S('r_wuy', 2), depth=dn)
    with jax.named_scope('wd_send0'):
        wd_send(0)

    for i, Z in enumerate((X, DY)):
        wait(wb.at[i], S('xg'[i] + 'bounce', 1))
    wait(vec_at, S('l_vec', 0))
    wait(vec_v.at[:, pl.ds(0, 3 * HB)], S('r_vec', 0))
    wait(bu_at, S('l_vec', 1))
    wait(bu_at, S('r_vec', 1))

    def norm_rows(buf, rows):
        xf = buf[rows, :].astype(F32)
        mean = jnp.sum(xf, axis=1, keepdims=True) * inv_w
        cen = xf - mean
        inv = lax.rsqrt(jnp.sum(cen * cen, axis=1, keepdims=True) * inv_w + LN_EPS)
        return cen, mean, inv

    def tok_of(s):
        return tau + s * (1 - 2 * tau)

    def phase1(k):
        @pl.when(k < NCH - 1)
        def _():
            with jax.named_scope('x_near'):
                x_near(k + 1)

        @pl.when(k == 1)
        def _():
            with jax.named_scope('wd_send1'):
                wd_send(1)
            send_own('g', dy_ref, DY, ('near',))

        @pl.when(k == 2)
        def _():
            send_own('g', dy_ref, DY, ('far',))

        @pl.when(k == NCH - 1)
        def _():
            with jax.named_scope('wd_relay0'):
                wd_relay(0)

        with jax.named_scope('x_far'):
            wait(reg(X, k, cf), S('xfar', k))
            d2d('x', X, k, cf, 'd2d')
        with jax.named_scope('x_opp'):
            wait(reg(X, k, co), S('xopp', k))
            d2d('x', X, k, co, 'd2d')
        rows = ds(k * BLK, BLK)
        with jax.named_scope('x_d2d'):
            wait(X.at[rp, rows, :], S('xd2d', k))

        @pl.when(k > 0)
        def _():
            for s in range(2):
                wait(wb.at[s], S('st', s))
        for s in range(2):
            copy(X.at[tok_of(s), rows, :], wb.at[s], S('ld', s))

        @pl.when(k == 0)
        def _():
            with jax.named_scope('wuo'):
                wait(wuq(do, 0), S('r_wuy', 2))
                wait(wuq(do, 1), S('r_wuy', 3))

        for s in range(2):
            wait(wb.at[s], S('ld', s))

            def ln(i):
                rr = ds(i * LROWS, LROWS)
                cen, _, inv = norm_rows(wb.at[s], rr)
                wb[s, rr, :] = (cen * inv * vec_v[0:1, :] + vec_v[1:2, :]).astype(BF16)
            with jax.named_scope('ln'):
                loop(BLK // LROWS, ln)
            copy(wb.at[s], XN.at[s, rows, :], S('st', s))

            def stored():
                wait(wb.at[2], S('st', 2))
                wait(wb.at[3], S('st', 3))
            if s:
                stored()
            else:
                pl.when(k > 0)(stored)

            def tile(n):
                cols = ds(s * o + n * NTW, NTW)
                acc = lax.dot_general(wb[s], wu_v[:, cols], NN, preferred_element_type=F32) + bu_v[0:1, cols]
                u = acc.astype(BF16)
                wb[2, :, cols] = u
                wb[3, :, cols] = gelu(u.astype(F32)).astype(BF16)
            with jax.named_scope('u_tiles'):
                loop((2 - s) * (FH // NTW), tile)
            copy(wb.at[2, :, pl.ds(0, FB)], U.at[s, rows, :], S('st', 2))
            copy(wb.at[3, :, pl.ds(0, FB)], A.at[s, rows, :], S('st', 3))
    loop(NCH, phase1)
    for i in range(4):
        wait(wb.at[i], S('st', i))

    def g_near_far(k):
        wait(reg(DY, k, cf), S('gfar', k))
        put(reg(DY, k, cf), reg(DY, k, cf), S('gs_rel', k), S('gopp', k), col=cn)
        d2d('g', DY, k, cf, 'd2d')
        wait(reg(DY, k, cn), S('gnear', k))
        d2d('g', DY, k, cn, 'd2d')

    def g_opp(k):
        wait(reg(DY, k, co), S('gopp', k))
        d2d('g', DY, k, co, 'd2o')
        wait(reg(DY, k, co), S('gd2o', k))

    def tile_y(lhs, col):
        return lax.dot_general(lhs, wd_v[:, dsm(col, NTW, NTW)], NN, preferred_element_type=F32)

    def tile_g(lhs, col):
        return lax.dot_general(lhs, wu_v[dsm(col, NTW, NTW), :], NT, preferred_element_type=F32)

    def give(p, src, tile, GOT):
        def blk(b):
            return src.at[0, dsm(rp * TH + b * BLK, BLK, BLK), :]
        copy(blk(0), wb.at[0, :, pl.ds(0, FB)], S('ld', 0))

        def step(b):
            wait(wb.at[b, :, pl.ds(0, FB)], S('ld', b))

            @pl.when(b == 0)
            def _():
                copy(blk(1), wb.at[1, :, pl.ds(0, FB)], S('ld', 1))

            def half(h):
                @pl.when(b == 1)
                def _():
                    wait(fb.at[h], S(p + 's_give', h))

                def n_tile(n):
                    fb[h, :, ds(n * NTW, NTW)] = tile(wb[b, :, :FB], h * HW + n * NTW)
                loop(HW // NTW, n_tile)
                put(fb.at[h], GOT.at[ds(b * BLK, BLK), ds(h * HW, HW)], S(p + 's_give', h), S(p + 'got', b), row=rp)
            loop(2, half)
        loop(2, step)

    def keep(p, src, tile, GOT, FAR, KEEP):
        def blk(b):
            return src.at[0, dsm(r * TH + b * BLK, BLK, BLK), :]
        copy(blk(0), wb.at[0, :, pl.ds(0, FB)], S('ld', 0))
        copy(blk(1), wb.at[1, :, pl.ds(0, FB)], S('ld', 1))
        for h in range(2):
            wait(fb.at[h], S(p + 's_give', h))

        def part(b, h):
            brow = ds(b * BLK, BLK)
            col0 = (1 - f + h * (2 * f - 1)) * HW
            out = (2 + b) * (1 - h) + h
            copy(GOT.at[brow, ds(col0, HW)], fb.at[0], S('ld', 2))

            @pl.when(jnp.logical_and(b == 1, h == 1))
            def _():
                wait(fb.at[1], S(p + 'keep'))

            def n_tile(n):
                fb[out, :, ds(n * NTW, NTW)] = tile(wb[b, :, :FB], col0 + n * NTW)
            loop(HW // NTW, n_tile)
            wait(fb.at[0], S('ld', 2))

            def add(i):
                rr = ds(i * ROWS, ROWS)
                fb[out, rr, :] = fb[out, rr, :] + fb[0, rr, :]
            loop(BLK // ROWS, add)

            @pl.when(h == 0)
            def _():
                put(fb.at[2 + b], FAR.at[brow, :], S(p + 's_far', b), S(p + 'far', b), col=cf)

            @pl.when(h == 1)
            def _():
                copy(fb.at[1], KEEP.at[brow, :], S(p + 'keep'))

        def step(b):
            with jax.named_scope('got'):
                wait(GOT.at[ds(b * BLK, BLK), :], S(p + 'got', b))
            wait(wb.at[b, :, pl.ds(0, FB)], S('ld', b))
            loop(2, lambda h: part(b, h))
        loop(2, step)
        wait(fb.at[1], S(p + 'keep'))

    def keep_end(p):
        for b in range(2):
            wait(fb.at[2 + b], S(p + 's_far', b))

    def place(p, out, b):
        dst = out.at[dsm(r * TH + b * BLK, BLK, BLK), :]
        mine, other = ob.at[b, :, ds(c_odd * HB, HB)], ob.at[b, :, ds((1 - c_odd) * HB, HB)]
        put(other, dst, S(p + 's_out', 2 * b), S(p + 'out'), col=cn, row=tau)

        @pl.when(r == tau)
        def _():
            copy(mine, dst, S(p + 'loc', b))

        @pl.when(r != tau)
        def _():
            put(mine, dst, S(p + 's_out', 2 * b + 1), S(p + 'out'), row=rp)

    def place_end(p, b):
        wait(ob.at[b, :, pl.ds(0, HB)], S(p + 's_out', 2 * b))

        @pl.when(r == tau)
        def _():
            wait(ob.at[b, :, pl.ds(0, HB)], S(p + 'loc', b))

        @pl.when(r != tau)
        def _():
            wait(ob.at[b, :, pl.ds(0, HB)], S(p + 's_out', 2 * b + 1))

    fcols = ds(f * HW, HW)

    def y_final(b):
        brow = ds(b * BLK, BLK)
        wait(YFAR.at[brow, :], S('yfar', b))
        copy(YFAR.at[brow, :], fb.at[0], S('ld', 0))
        copy(YKEEP.at[brow, :], fb.at[1], S('ld', 1))
        copy(X.at[tau, dsm(r * TH + b * BLK, BLK, BLK), fcols], wb.at[0, :, pl.ds(0, HW)], S('ld', 2))
        wait(fb.at[0], S('ld', 0))
        wait(fb.at[1], S('ld', 1))
        wait(wb.at[0, :, pl.ds(0, HW)], S('ld', 2))

        def fin(i):
            rr = ds(i * ROWS, ROWS)
            ob[b, rr, :] = (wb[0, rr, :HW].astype(F32) + (fb[0, rr, :] + fb[1, rr, :]) + vec_v[2:3, fcols]).astype(BF16)
        loop(BLK // ROWS, fin)
        place('y', y_out, b)

    def da_load(k, s, slot):
        rows = ds(k * BLK, BLK)
        copy(DY.at[tok_of(s), rows, :], wb.at[slot], S('ld', slot))
        copy(U.at[s, rows, :], wb.at[2 + slot, :, pl.ds(0, FB)], S('ld', 2 + slot))

    def da_block(k, s, slot):
        rows = ds(k * BLK, BLK)
        wait(wb.at[slot], S('ld', slot))
        wait(wb.at[2 + slot, :, pl.ds(0, FB)], S('ld', 2 + slot))

        def tile(n):
            cols = ds(s * o + n * NTW, NTW)
            da = lax.dot_general(wb[slot], wd_v[cols, :], NT, preferred_element_type=F32)
            du = (da * gelu_slope(wb[2 + slot, :, cols].astype(F32))).astype(BF16)
            wb[2 + slot, :, cols] = du
            db_v[s, :, cols] += jnp.sum(du.astype(F32).reshape(BLK // 8, 8, NTW), axis=0)
        loop((2 - s) * (FH // NTW), tile)
        copy(wb.at[2 + slot, :, pl.ds(0, FB)], DU.at[s, rows, :], S('st', slot))

    def da_stored(slot):
        wait(wb.at[2 + slot, :, pl.ds(0, FB)], S('st', slot))

    def rows_of(kb):
        return ds(lax.rem(kb, NCH) * BLK, BLK), lax.div(kb, NCH)

    d_col = (c, cn, cf, co)

    NB, NSLOT = 2 * NCH, 4

    def k_loop(load, use, width):
        for kb in range(NSLOT - 1):
            load(kb, kb)

        def step(kb):
            slot = lax.rem(kb, NSLOT)

            @pl.when(kb + NSLOT - 1 < NB)
            def _():
                load(kb + NSLOT - 1, lax.rem(kb + NSLOT - 1, NSLOT))
            wait(wb.at[slot, :, pl.ds(0, width)], S('ld', slot))
            use(slot)
        loop(NB, step)

    def dwd_pass(js):
        def load(kb, slot):
            rows, s = rows_of(kb)
            copy(A.at[s, rows, ds(o, FH)], wb.at[slot, :, pl.ds(0, FH)], S('ld', slot))
            for i, j in enumerate(js):
                copy(DY.at[tok_of(s), rows, ds(d_col[j] * HB, HB)], wb.at[slot, :, pl.ds(FH + i * HB, HB)], S('ld', slot))

        def use(slot):
            for i, j in enumerate(js):
                for m in range(2):
                    mm = slice(m * FH // 2, (m + 1) * FH // 2)
                    accD[j, mm, :] += lax.dot_general(wb[slot, :, mm], wb[slot, :, FH + i * HB:FH + (i + 1) * HB], TN, preferred_element_type=F32)
        for j in js:
            accD[j] = jnp.zeros((FH, HB), F32)
        k_loop(load, use, FH + len(js) * HB)

    def dwd_opp(j):
        put(accD.at[j, dsm(do * QF, QH, QH), :], r1D.at[j], S('d_so', 2 * j), S('d_r', 2 * j), depth=dn)
        put(accD.at[j, dsm(do * QF + QH, QH, QH), :], r2D.at[j], S('d_so', 2 * j + 1), S('d_r', 2 * j + 1), depth=df)

    def dwd_a(j):
        wait(r1D.at[j], S('d_r', 2 * j))
        rr = dsm(df * QF, QH, QH)
        accD[j, rr, :] += r1D[j]
        put(accD.at[j, ds(df * QF, QF), :], PFD.at[j], S('d_sa', 2 * j), S('d_p', 2 * j), depth=df)
        wait(r2D.at[j], S('d_r', 2 * j + 1))
        rr = dsm(dn * QF + QH, QH, QH)
        accD[j, rr, :] += r2D[j]
        put(accD.at[j, ds(dn * QF, QF), :], PND.at[j], S('d_sa', 2 * j + 1), S('d_p', 2 * j + 1), depth=dn)

    def dwd_rows(q, h, dd):
        return dsm((2 * q + h) * FH + dd * QF, QF, QF)

    def dwd_b(j):
        wait(PFD.at[j], S('d_p', 2 * j))
        wait(PND.at[j], S('d_p', 2 * j + 1))
        wait(PFD.at[j], S('d_sa', 2 * j))
        wait(PND.at[j], S('d_sa', 2 * j + 1))
        pf, pn = accD.at[j, ds(df * QF, QF), :], accD.at[j, ds(dn * QF, QF), :]
        copy(PFD.at[j], pf, S('ld', 6))
        copy(PND.at[j], pn, S('ld', 7))
        wait(pf, S('ld', 6))
        wait(pn, S('ld', 7))
        finD[j] = (accD[j, ds(d * QF, QF), :] + (pf[...] + pn[...])).astype(BF16)
        dst = gwd_out.at[dwd_rows(c_odd, r, d), :]
        if j:
            put(finD.at[j], dst, S('d_sf', j), S('d_out'), col=d_col[j], row=f)
        else:
            @pl.when(r == f)
            def _():
                copy(finD.at[0], dst, S('d_out'))

            @pl.when(r != f)
            def _():
                put(finD.at[0], dst, S('d_sf', 0), S('d_out'), row=rp)

    def gwd(i, dd, half=None):
        if half is None:
            return gwd_out.at[dsm(i * FH + dd * QF, QF, QF), :]
        return gwd_out.at[dsm(i * FH + dd * QF + half * QH, QH, QH), :]

    def gwd_send():
        wait(gwd_out.at[pl.ds(0, 4 * QF), :], S('d_out'))
        for i in range(4):
            put(gwd(i, d), gwd(i, d), S('d_sy', i), S('d_y', 0), depth=dn)
            put(gwd(i, d), gwd(i, d), S('d_sy', 4 + i), S('d_y', 1), depth=df)

    def gwd_relay():
        wait(gwd_out.at[pl.ds(0, 4 * QF), :], S('d_y', 0))
        for i in range(4):
            put(gwd(i, dn, 1), gwd(i, dn, 1), S('d_sr', i), S('d_o', 1), depth=df)
        wait(gwd_out.at[pl.ds(0, 4 * QF), :], S('d_y', 1))
        for i in range(4):
            put(gwd(i, df, 0), gwd(i, df, 0), S('d_sr', 4 + i), S('d_o', 0), depth=dn)

    def dwu_pass(dds):
        def load(kb, slot):
            rows, s = rows_of(kb)
            copy(DU.at[s, rows, ds(o, FH)], wb.at[slot, :, pl.ds(0, FH)], S('ld', slot))
            for i, dd in enumerate(dds):
                copy(XN.at[s, rows, ds(dd * DQ, DQ)], wb.at[slot, :, pl.ds(FH + i * DQ, DQ)], S('ld', slot))

        def use(slot):
            for i, dd in enumerate(dds):
                for m in range(2):
                    mm = slice(m * FH // 2, (m + 1) * FH // 2)
                    accU[dd, :, mm] += lax.dot_general(wb[slot, :, FH + i * DQ:FH + (i + 1) * DQ], wb[slot, :, mm], TN, preferred_element_type=F32)
        for dd in dds:
            accU[dd] = jnp.zeros((DQ, FH), F32)
        k_loop(load, use, FH + len(dds) * DQ)

    def dwu_opp():
        put(accU.at[do, pl.ds(0, DH), :], r1U, S('u_so', 0), S('u_r', 0), depth=dn)
        put(accU.at[do, pl.ds(DH, DH), :], r2U, S('u_so', 1), S('u_r', 1), depth=df)

    def dwu_a():
        wait(r1U, S('u_r', 0))
        accU[df, :DH, :] += r1U[...]
        put(accU.at[df], PFU, S('u_sa', 0), S('u_p', 0), depth=df)
        wait(r2U, S('u_r', 1))
        accU[dn, DH:, :] += r2U[...]
        put(accU.at[dn], PNU, S('u_sa', 1), S('u_p', 1), depth=dn)

    def dwu_b():
        wait(PFU, S('u_p', 0))
        wait(PNU, S('u_p', 1))
        pf, pn = fb.at[0, :, pl.ds(0, FH)], fb.at[1, :, pl.ds(0, FH)]
        copy(PFU, pf, S('ld', 6))
        copy(PNU, pn, S('ld', 7))
        wait(pf, S('ld', 6))
        wait(pn, S('ld', 7))

        def fin(i):
            rr = ds(i * ROWS, ROWS)
            wb[3, rr, HW:HW + FH] = (accU[d, rr, :] + (fb[0, rr, :FH] + fb[1, rr, :FH])).astype(BF16)
        loop(DQ // ROWS, fin)
        dst = gwu_out.at[ds(d_odd * DQ, DQ), ds(r * FH, FH)]
        put(finU, dst, S('u_sf', 0), S('u_out', 1), depth=dn, row=dh)
        put(finU, dst, S('u_sf', 1), S('u_out', 2), depth=df, row=dh)

        @pl.when(r == dh)
        def _():
            copy(finU, dst, S('u_out', 0))

        @pl.when(r != dh)
        def _():
            put(finU, dst, S('u_sf', 2), S('u_out', 0), row=rp)

    def gwu(start, size):
        return gwu_out.at[dsm(start, size, size), :]

    def gwu_relay():
        @pl.when(r == dh)
        def _():
            wait(gwu(lax.rem(dn, 2) * DQ, DQ), S('u_out', 1))
            part = gwu(lax.rem(dn, 2) * DQ + DH, DH)
            put(part, part, S('u_sr'), S('u_o', 1), depth=df)

        @pl.when(r != dh)
        def _():
            wait(gwu(lax.rem(df, 2) * DQ, DQ), S('u_out', 2))
            part = gwu(lax.rem(df, 2) * DQ, DH)
            put(part, part, S('u_sr'), S('u_o', 0), depth=dn)

    def gwu_end():
        @pl.when(r == dh)
        def _():
            wait(gwu(d_odd * DQ, DQ), S('u_out', 0))

        @pl.when(r != dh)
        def _():
            wait(gwu(0, DH), S('u_o', 0))
            wait(gwu(0, DH), S('u_o', 1))

    lane = lax.broadcasted_iota(jnp.int32, (LROWS, 128), 1)

    def dx_a(b):
        brow = ds(b * BLK, BLK)
        trow = dsm(r * TH + b * BLK, BLK, BLK)
        wait(GFAR.at[brow, :], S('dfar', b))
        copy(GFAR.at[brow, :], fb.at[0], S('ld', 0))
        copy(GKEEP.at[brow, :], fb.at[1], S('ld', 1))
        copy(X.at[tau, trow, :], wb.at[b], S('ld', 2))
        copy(DY.at[tau, trow, fcols], wb.at[2 + b, :, pl.ds(0, HW)], S('ld', 3))
        wait(fb.at[0], S('ld', 0))
        wait(fb.at[1], S('ld', 1))
        wait(wb.at[b], S('ld', 2))
        wait(wb.at[2 + b, :, pl.ds(0, HW)], S('ld', 3))

        def rows_step(i):
            rr = ds(i * LROWS, LROWS)
            _, mean, inv = norm_rows(wb.at[b], rr)
            xhat = (wb[b, rr, fcols].astype(F32) - mean) * inv
            dxn = fb[0, rr, :] + fb[1, rr, :]
            fb[2 + b, rr, :] = dxn
            gh = dxn * vec_v[0:1, fcols]
            s0 = jnp.sum(gh, axis=1, keepdims=True)
            s1 = jnp.sum(gh * xhat, axis=1, keepdims=True)
            srow = rr
            st_v[srow, :] = jnp.where(lane < 64, s0, s1)
            ms_v[srow, :] = jnp.where(lane < 64, mean, inv)
            p1 = dxn * xhat
            cs_v[0] += jnp.sum(p1.reshape(LROWS // 8, 8, HW), axis=0)
            cs_v[1] += jnp.sum(dxn.reshape(LROWS // 8, 8, HW), axis=0)
        loop(BLK // LROWS, rows_step)

    SB = min(BLK, 128)
    NS = BLK // SB

    def stats_send(b):
        for t in range(NS):
            tr = st_v[t * SB:(t + 1) * SB, :].T
            sx_v[b, t:t + 1, :SB] = tr[0:1, :]
            sx_v[b, NS + t:NS + t + 1, :SB] = tr[64:65, :]
        put(sx_v.at[b], sr_v.at[b], S('s_st', b), S('r_st', b), col=cf)

    def stats_recv(b):
        wait(sr_v.at[b], S('r_st', b))
        for t in range(NS):
            for i in range(2):
                row = (sx_v[b, i * NS + t:i * NS + t + 1, :SB] + sr_v[b, i * NS + t:i * NS + t + 1, :SB]) * inv_w
                st2_v[i, t * SB:(t + 1) * SB, :] = jnp.broadcast_to(row, (128, SB)).T

    def dx_b(b):
        def rows_step(i):
            rr = ds(i * ROWS, ROWS)
            srow = rr
            mean, inv = ms_v[srow, 0:1], ms_v[srow, 64:65]
            xhat = (wb[b, rr, fcols].astype(F32) - mean) * inv
            gh = fb[2 + b, rr, :] * vec_v[0:1, fcols]
            dx = wb[2 + b, rr, :HW].astype(F32) + inv * (gh - st2_v[0, srow, 0:1] - xhat * st2_v[1, srow, 0:1])
            ob[b, rr, :] = dx.astype(BF16)
        loop(BLK // ROWS, rows_step)
        place('d', dx_out, b)

    def sums():
        cw = jnp.sum(cs_v[...], axis=1)
        for i in range(2):
            for q in range(2):
                @pl.when(c_odd == q)
                def _():
                    sum_v[0, :, i * HB:(i + 1) * HB] = cw[i:i + 1, q * HB:(q + 1) * HB]
                    sum_v[1, :, i * HB:(i + 1) * HB] = cw[i:i + 1, (1 - q) * HB:(2 - q) * HB]
        near = sum_v.at[1, :, pl.ds(0, 2 * HB)]
        near_in = sumr_v.at[0, :, pl.ds(0, 2 * HB)]
        put(near, near_in, S('s_sum', 0), S('r_sum', 0), col=cn)
        sum_v[0, :, 2 * HB:2 * HB + FB] = jnp.zeros((1, FB), F32)
        sum_v[0, :, dsm(2 * HB + r * FH, FH, HB)] = jnp.sum(db_v[0, :, ds(o, FH)] + db_v[1, :, ds(o, FH)], axis=0, keepdims=True)
        sum_v[0, :, 2 * HB + FB:] = jnp.sum(bd_v[...], axis=0, keepdims=True)
        wait(near_in, S('r_sum', 0))
        sum_v[2, :, :2 * HB] = sum_v[0, :, :2 * HB] + sumr_v[0, :, :2 * HB]
        sum_v[2, :, 2 * HB:] = sum_v[0, :, 2 * HB:]
        for i, dev in enumerate((dict(row=rp), dict(depth=dn), dict(depth=df))):
            put(sum_v.at[2 + i], sumr_v.at[1 + i], S('s_sum', 1 + i), S('r_sum', 1 + i), **dev)
            wait(sumr_v.at[1 + i], S('r_sum', 1 + i))
            sum_v[3 + i] = sum_v[2 + i] + sumr_v[1 + i]
        copy(sum_v.at[5], sum_out, S('l_small', 0))

    scope = jax.named_scope

    def g_ready(k):
        wait(DY.at[rp, ds(k * BLK, BLK), pl.ds(0, 3 * HB)], S('gd2d', k))

    def da_t(k):
        with scope('g_opp'):
            g_opp(k)
        slot = lax.rem(k, 2)

        @pl.when(k > 1)
        def _():
            da_stored(slot)
        da_load(k, 0, slot)
        with scope('da_t'):
            da_block(k, 0, slot)

    def da_n(k):
        slot = lax.rem(k, 2)

        @pl.when(k < NCH - 1)
        def _():
            @pl.when(k > 0)
            def _():
                da_stored(1 - slot)
            da_load(k + 1, 1, 1 - slot)
        with scope('da_n'):
            da_block(k, 1, slot)

    def da_end():
        da_stored(0)
        da_stored(1)

    with scope('g01'):
        loop(2, g_near_far)
    with scope('wd_relay1'):
        wd_relay(1)
    with scope('wd_wait'):
        for g in range(2):
            for i in range(2, 4):
                wait(wd_bytes(g, QH), S('r_wdy', 4 * g + i))
    with scope('y_give'):
        give('y', A, tile_y, YGOT)
    with scope('g2'):
        g_near_far(2)
    with scope('y_keep'):
        keep('y', A, tile_y, YGOT, YFAR, YKEEP)
    with scope('g3'):
        g_near_far(3)
    with scope('g_ready'):
        loop(NCH, g_ready)
    with scope('dwd_0'):
        dwd_pass((0,))
        dwd_opp(0)
    with scope('dwd_12'):
        dwd_pass((1, 2))
        dwd_opp(1)
        dwd_opp(2)
    with scope('dwd_a0'):
        dwd_a(0)
    loop(NCH, da_t)
    da_end()
    with scope('dwd_a12'):
        dwd_a(1)
        dwd_a(2)
    with scope('dwd_3'):
        dwd_pass((3,))
        dwd_opp(3)
    with scope('dwd_b0'):
        dwd_b(0)
    with scope('d_give'):
        give('d', DU, tile_g, GGOT)
    with scope('dwd_a3'):
        dwd_a(3)
    with scope('da_n_all'):
        da_load(0, 1, 0)
        loop(NCH, da_n)
        da_end()
    with scope('dwd_b12'):
        dwd_b(1)
        dwd_b(2)
    with scope('dwu_01'):
        dwu_pass((do, df))
        dwu_opp()
    with scope('keep_end_y'):
        keep_end('y')
    with scope('d_keep'):
        keep('d', DU, tile_g, GGOT, GFAR, GKEEP)
    with scope('dwd_b3'):
        dwd_b(3)
    with scope('dwu_23'):
        dwu_pass((dn, d))
    with scope('dwu_a'):
        dwu_a()
    with scope('gwd_send'):
        gwd_send()
    for b in range(2):
        with scope('y_final'):
            y_final(b)
    with scope('gwd_relay'):
        gwd_relay()
    with scope('dwu_b'):
        dwu_b()
    with scope('keep_end_d'):
        keep_end('d')
    for b in range(2):
        with scope('place_end_y'):
            place_end('y', b)
        with scope('dx_a'):
            dx_a(b)
        with scope('stats'):
            stats_send(b)
            stats_recv(b)
        with scope('dx_b'):
            dx_b(b)
        if b == 0:
            with scope('gwu_relay'):
                gwu_relay()
    with scope('sums'):
        sums()

    with scope('gwu_end'):
        gwu_end()
    wait(gwd_out.at[pl.ds(0, 4 * QH), :], S('d_o', 0))
    wait(gwd_out.at[pl.ds(0, 4 * QH), :], S('d_o', 1))
    for p, out in (('y', y_out), ('d', dx_out)):
        @pl.when(r == tau)
        def _():
            wait(out.at[pl.ds(0, TH), :], S(p + 'out'))

        @pl.when(r != tau)
        def _():
            wait(out, S(p + 'out'))
    wait(sum_out, S('l_small', 0))
    for b in range(2):
        place_end('d', b)
    for b in range(2):
        wait(sx_v.at[b], S('s_st', b))
    wait(sum_v.at[1, :, pl.ds(0, 2 * HB)], S('s_sum', 0))
    for i in range(3):
        wait(sum_v.at[2 + i], S('s_sum', 1 + i))
    wait(wun, S('s_wun'))

    @pl.when(r == f)
    def _():
        for s in range(2):
            wait(wd_dst(0, c), S('s_wd0', s))
    for i in range(4):
        wait(wd_dst(0, c), S('s_wdx', i))
    wait(wu_own, S('s_wu'))
    for i in range(3):
        wait(vec_at, S('s_vec', i))
    wait(bu_at, S('s_vec', 3))
    for s in range(2):
        wait(wd_dst(s, cf), S('s_wdr', s))
    for i in range(2):
        wait(wuq(d), S('s_wuy', i))
        wait(wuq(d, 0), S('s_wuy', 2 + i))
    for i in range(16):
        wait(wdq(0, d, c), S('s_wdy', i))
        wait(wdq(0, d, c, 0), S('s_wdy', 16 + i))

    def sends(k):
        for z, Z in (('x', X), ('g', DY)):
            for n in ('s_near', 's_far', 's_rel'):
                wait(reg(Z, k, c), S(z + n, k))
            wait(Z.at[r, ds(k * BLK, BLK), :], S(z + 's_d2d', k))
    loop(NCH, sends)
    for i in range(8):
        wait(r1D.at[0], S('d_so', i))
        wait(gwd(0, d), S('d_sy', i))
        wait(gwd(0, d, 0), S('d_sr', i))
    for j in range(1, 4):
        wait(finD.at[j], S('d_sf', j))

    @pl.when(r != f)
    def _():
        wait(finD.at[0], S('d_sf', 0))
    for i in range(2):
        wait(r1U, S('u_so', i))
        wait(PFU, S('u_sa', i))
        wait(finU, S('u_sf', i))

    @pl.when(r != dh)
    def _():
        wait(finU, S('u_sf', 2))
    wait(gwu(0, DH), S('u_sr'))


def block_kernel(x, dy, wu, wd, vec, bu):
    (TK, HB), FH = x.shape, wu.shape[1] // 2
    W, HW, TH, BLK, QF, FB = 4 * HB, 2 * HB, TK // 2, TK // NCH, FH // 4, 2 * FH
    assert FB <= W and FH <= HW and W // 4 <= BLK and QF <= BLK
    sd = jax.ShapeDtypeStruct
    NS = BLK // min(BLK, 128)
    outs = [sd((TK, HB), BF16), sd((TK, HB), BF16), sd((W // 2, FB), BF16), sd((4 * FH, HB), BF16), sd((1, 3 * HB + FB), F32)]
    n_out = len(outs)
    outs += [sd((2, TK, W), BF16)] * 3 + [sd((2, TK, FB), BF16)] * 3
    outs += [sd((TH, W), F32), sd((TH, HW), F32), sd((TH, HW), F32)] * 2
    outs += [sd((4, QF, HB), F32)] * 2 + [sd((W // 4, FH), F32)] * 2
    V = pltpu.VMEM
    scratch = [
        V((W, FB), BF16), V((FB, W), BF16), V((4, FH, HB), F32), V((4, W // 4, FH), F32),
        V((4, FH // 8, HB), F32), V((4, FH // 8, HB), F32), V((W // 8, FH), F32), V((W // 8, FH), F32),
        V((8, W), F32), V((8, FB), F32), V((4, BLK, W), BF16), V((4, BLK, HW), F32), V((2, BLK, HW), BF16),
        V((4, QF, HB), BF16), V((2, 8, FB), F32), V((2, 8, HW), F32),
        V((BLK, 128), F32), V((BLK, 128), F32), V((2, BLK, 128), F32), V((2, 2 * NS, 128), F32), V((2, 2 * NS, 128), F32),
        V((8, HB), F32), V((6, 1, 3 * HB + FB), F32), V((4, 1, 3 * HB + FB), F32),
        pltpu.SemaphoreType.DMA((N_SEM,)),
    ]
    res = pl.pallas_call(
        functools.partial(body, (TK, HB, FH)),
        out_shape=outs,
        in_specs=[pl.BlockSpec(memory_space=pl.ANY)] * 6,
        out_specs=[pl.BlockSpec(memory_space=pl.ANY)] * len(outs),
        scratch_shapes=scratch,
        compiler_params=pltpu.CompilerParams(collective_id=0, has_side_effects=True, vmem_limit_bytes=67043328),
        name='mlp_block',
    )(x, dy, wu, wd, vec, bu)
    return res[:n_out]


def solution(mesh):
    assert (mesh.shape['col'], mesh.shape['row'], mesh.shape['depth']) == (4, 2, 4)
    tok_spec = P(('dp', 'depth', 'row'), 'col')
    vec_spec = P('col')
    mat_spec = P('row', 'col')
    grad_vec = P(('dp', 'col'))
    grad_mat = P(('dp', 'row'), 'col')
    def local_pass(x_blk, gamma_blk, beta_blk, w_up_blk, b_up_blk, w_down_blk, b_down_blk, dy_blk):
        hb, fb = x_blk.shape[1], w_up_blk.shape[1]
        vec = jnp.stack([gamma_blk, beta_blk, b_down_blk.astype(F32)] + [jnp.zeros_like(gamma_blk)] * 5)
        bu = jnp.broadcast_to(b_up_blk.astype(F32)[None], (8, fb))
        y_blk, dx_blk, grad_w_up, grad_w_down, sums = block_kernel(x_blk, dy_blk, w_up_blk, w_down_blk, vec, bu)
        sums = sums[0]
        return (y_blk, dx_blk, sums[:hb], sums[hb:2 * hb], grad_w_up, sums[2 * hb:2 * hb + fb], grad_w_down, sums[2 * hb + fb:])

    return jax.shard_map(
        local_pass,
        mesh=mesh,
        in_specs=(tok_spec, vec_spec, vec_spec, mat_spec, vec_spec, mat_spec, vec_spec, tok_spec),
        out_specs=(tok_spec, tok_spec, grad_vec, grad_vec, grad_mat, grad_vec, grad_mat, grad_vec),
        check_vma=False,
    )
```

time: 821 us -> 512 us (0.62)
  Pallas kernels: 773 us -> 493 us
  blocking collectives: 23.6 us -> 0 us
    pallas_call x1, Pallas kernels: 773 us -> 493 us  [block_kernel(): pl.pallas_call(functools.partial(body, (TK, HB, FH)), out_shape=outs, in_...]
    psum x1 -> x0, blocking collectives: 23.6 us -> none  [local_pass(): lax.psum(jnp.concatenate([cols[0], cols[1], db_up, db_down]), ('depth', '...]
  transfers between devices with their start and end apart: 1 -> 0, of which waited for: 0 -> 0; matrix products, arithmetic and copies ran while one was open for 0% -> 0% of each run, Pallas kernels for 0% -> 0%
where the time goes in v2:
time: 512 us; the launch traced here: 510 us
  Pallas kernels  493 us (96%)
  local copies, waits for them, and re-layouts  15.6 us (3%)
    pallas_call x1, Pallas kernels, block_kernel(): pl.pallas_call(functools.partial(body, (TK, HB, FH)), out_shape=outs, in_...  493 us
    unnamed x10, local copies, waits for them, and re-layouts  10.2 us

profile of v2, /device:TPU:96, one launch (start us, length us, event | category | flops | bytes accessed | tf_op | source)
XLA Modules:
  0.0 510.4 jit_solution(6323351027156450283)
XLA Ops:
  0.6 0.7 stack.24
  1.3 1.3 stack.23.vec_ref
  2.6 1.3 broadcast_in_dim.2.bu_ref
  4.0 493.5 %mlp_block.1 = (bf16[2048,512]{1,0:T(8,128)(2,1)}, bf16[2048,512]{1,0:T(8,128)(2,1)}, bf16[1024,2048]{1,0:T(8,128)(2,1)}, bf16[4096,512]{1,0:T(8,128)(2,1)}, f32...) custom-call(bf16[2048,512]{1,0:T(8,128)(2,1)} %x_ref.1, ...), custom_call_target="tpu_custom_call" | custom-call | tf_op jit(solution)/shard_map/mlp_block/pallas_call | solution.py:969
  497.4 0.0 copy-start.2
  497.4 1.4 fusion
  498.9 1.3 slice.28
  500.2 0.0 copy-start.1
  500.2 3.2 copy.20
  503.4 0.0 copy-done.2
  503.4 1.3 copy.21
  504.7 0.0 copy-done.1
  504.7 0.0 copy-start
  504.7 2.1 copy.22
  506.8 1.6 copy-done
  508.4 2.0 copy.23
  (2 shorter events, 0.0 us)
Async XLA Ops:
  497.4 5.9 %copy-start.2 = (bf16[2048,512]{1,0:T(8,128)(2,1)S(1)}, bf16[2048,512]{1,0:T(8,128)(2,1)}, u32[]{:S(2)}) copy-start(bf16[2048,512]{1,0:T(8,128)(2,1)} %get-tuple-element.30) | copy-start | bytes 6291460
  500.2 4.5 copy-start.1
  504.7 3.7 copy-start
